TPU v7x, 256 devices: a whole 4x4x8 slice. The times are simulated.
256 devices in a mesh: sub: 64 (over z, y, core), panel: 4 (over x).
Axes of the slice: x: 4, y: 4, z: 8, core: 2. Of those that a mesh axis runs over, the one named last changes fastest.
Arguments:
- interior_factor: float32 [512, 512, 512], P('sub'), may hold values from -1 to 3, as said below
- coupling: bfloat16 [512, 512, 2048], P('sub', None, 'panel'), may hold values from -1 to 1
- interface_diag: float32 [65536], P(('sub', 'panel')), may hold values from 0.5 to 4
- interface_column: float32 [65536, 128], P(('sub', 'panel')), may hold values from -1.8 to 1.8
- block_map: int32 [512, 16], replicated, may hold values from 0 to 511, as said below
- pair_pattern: int32 [512, 8], P('sub'), may hold values 0 or 1
Outputs:
- assembled: float32 [65536, 1024], P(('sub', 'panel'))
- factored: float32 [65536, 1024], P(('sub', 'panel'))
Inputs may be any that keep to these rules, and one draw needn't show every extreme that they name: Local block a of a subdomain has its owner block_map // 8 and its position block_map % 8 among that owner's blocks, one of the 2 positions from (a // 4) * 2. Blocks a and b of one subdomain with a % 4 == b % 4 have the same owner. The 32 block groups of the subdomains of one index of sub go at most 1 to one owner, and some owner gets exactly 1 of them. `interior_factor`: lower triangular; the diagonal lies between 1 and 3.
All inputs are finite; a program needn't handle non-finite values. No bound on the sum of `pair_pattern` on one device may be relied on, other than what follows from the above.
Results may differ from a plain program's by a relative error of at most 0.0006.
Values may be sent and summed in bfloat16 or wider, within the bound.
A program may use at most 128 MiB of HBM per device.

v0:
```python
import jax
import jax.numpy as jnp
from jax import lax
from jax.sharding import PartitionSpec as P

BLK = 128
OWN = 8


def partner(value, axis, apart):
    mask = 2**apart
    pairs = [(source, source ^ mask) for source in range(lax.axis_size(axis))]
    return lax.ppermute(value, axis, pairs)


def rank_within(owner_ids):
    length = owner_ids.shape[-1]
    same_owner = owner_ids[..., :, None] == owner_ids[..., None, :]
    earlier = jnp.arange(length)[None, :] < jnp.arange(length)[:, None]
    return jnp.sum(jnp.logical_and(same_owner, earlier), axis=-1)


def pair_products(left_blocks, right_blocks):
    return jnp.einsum(
        "snti,sntj->stij", left_blocks, right_blocks, preferred_element_type=jnp.float32
    )


def lower_solve(pivot, column):
    return lax.linalg.triangular_solve(pivot, column.T, left_side=True, lower=True).T


def outer_product(left_rows, right_rows):
    return jnp.einsum("ik,jk->ij", left_rows, right_rows, precision=lax.Precision.HIGHEST)


def blocked_solve(factor, right_side):
    interior = factor.shape[1]
    block_total = interior // BLK
    identity = jnp.broadcast_to(jnp.eye(BLK, dtype=jnp.float32), (factor.shape[0], BLK, BLK))
    inverses = []
    for block in range(block_total):
        diag_block = factor[:, block * BLK : (block + 1) * BLK, block * BLK : (block + 1) * BLK]
        inverses.append(
            lax.linalg.triangular_solve(diag_block, identity, left_side=True, lower=True)
        )
    solved_parts = []
    for block in range(block_total):
        remainder = right_side[:, block * BLK : (block + 1) * BLK]
        if block > 0:
            earlier = jnp.concatenate(solved_parts, axis=1)
            strip = factor[:, block * BLK : (block + 1) * BLK, : block * BLK]
            remainder = remainder - jnp.einsum(
                "sik,skm->sim", strip, earlier, precision=lax.Precision.HIGHEST
            )
        solved_parts.append(
            jnp.einsum("sik,skm->sim", inverses[block], remainder, precision=lax.Precision.HIGHEST)
        )
    return jnp.concatenate(solved_parts, axis=1)


def per_device(
    interior_factor, coupling, interface_diag, interface_column, block_map, pair_pattern
):
    sub_count = lax.axis_size("sub")
    panel_count = lax.axis_size("panel")
    sub_index = lax.axis_index("sub")
    panel_index = lax.axis_index("panel")
    sub_local = coupling.shape[0]
    interior = coupling.shape[1]
    local_blocks = block_map.shape[1]
    groups = local_blocks // panel_count
    pair_offset = local_blocks // 2
    panel_rows = OWN // panel_count
    per_owner = max(1, groups * sub_local // sub_count)
    slot_total = sub_count * per_owner
    partner_bit = panel_count.bit_length() - 2
    solved = blocked_solve(interior_factor, coupling.astype(jnp.float32))
    w_local = solved.astype(jnp.bfloat16)
    w_blocks = w_local.reshape(sub_local, interior, groups, BLK)
    upper_half = (panel_index >= panel_count // 2).astype(jnp.int32)
    half_width = groups // 2
    outgoing_cols = lax.dynamic_slice_in_dim(w_blocks, (1 - upper_half) * half_width, half_width, 2)
    incoming = partner(
        outgoing_cols.reshape(sub_local, interior, half_width * BLK), "panel", partner_bit
    )
    own_part = lax.dynamic_slice_in_dim(w_blocks, upper_half * half_width, half_width, 2)
    computed = pair_products(own_part, incoming.reshape(sub_local, interior, half_width, BLK))
    mirrored = jnp.swapaxes(
        partner(computed.astype(jnp.bfloat16), "panel", partner_bit).astype(computed.dtype), 2, 3
    )
    cross_tiles = jnp.where(
        upper_half == 0,
        jnp.concatenate([computed, mirrored], axis=1),
        jnp.concatenate([mirrored, computed], axis=1),
    )
    pair_rows = (panel_index * groups + jnp.arange(groups, dtype=jnp.int32)) % pair_offset
    linked = jnp.take(pair_pattern, pair_rows, axis=1).astype(jnp.float32)
    cross_tiles = cross_tiles * linked[:, :, None, None]
    diagonal = pair_products(w_blocks, w_blocks)
    row_tiles = jnp.stack([diagonal, cross_tiles], axis=2)
    row_tiles = row_tiles.reshape(sub_local * groups, 2, BLK, BLK)
    own_map = lax.dynamic_slice(
        block_map, (sub_index * sub_local, panel_index * groups), (sub_local, groups)
    )
    owners = (own_map // OWN).reshape(-1)
    slot_ids = owners * per_owner + rank_within(owners)
    slot_match = (slot_ids[:, None] == jnp.arange(slot_total, dtype=jnp.int32)[None, :]).astype(
        jnp.int32
    )
    source = jnp.argmax(slot_match, axis=0)
    filled = jnp.max(slot_match, axis=0).astype(jnp.float32)
    received = lax.all_to_all(
        jnp.take(row_tiles, source, axis=0) * filled[:, None, None, None],
        "sub",
        split_axis=0,
        concat_axis=0,
        tiled=True,
    )
    row_map = lax.dynamic_slice_in_dim(block_map, panel_index * groups, groups, 1)
    partner_start = (panel_index + panel_count // 2) % panel_count * groups
    partner_map = lax.dynamic_slice_in_dim(block_map, partner_start, groups, 1)
    owners = (row_map // OWN).reshape(sub_count, sub_local * groups)
    rank_order = rank_within(owners)
    senders = jnp.arange(sub_count, dtype=jnp.int32)[:, None]
    slot_index = (senders * per_owner + rank_order) * 2
    position = (row_map % OWN).reshape(sub_count, -1)
    partner_pos = (partner_map % OWN).reshape(sub_count, -1)
    row_offset = (position - panel_index * panel_rows) * OWN
    targets = jnp.stack([row_offset + position, row_offset + partner_pos], axis=-1).reshape(-1)
    sources = jnp.stack([slot_index, slot_index + 1], axis=-1).reshape(-1)
    wanted = jnp.repeat((owners == sub_index).reshape(-1), 2)
    hit_rows = jnp.logical_and(
        jnp.arange(panel_rows * OWN, dtype=jnp.int32)[:, None] == targets[None, :], wanted[None, :]
    ).astype(jnp.float32)
    hit_cols = (sources[:, None] == jnp.arange(slot_total * 2, dtype=jnp.int32)[None, :]).astype(
        jnp.float32
    )
    landed = jnp.dot(
        jnp.dot(hit_rows, hit_cols, precision=lax.Precision.HIGHEST),
        received.reshape(slot_total * 2, BLK * BLK),
        precision=lax.Precision.HIGHEST,
    )
    assembled = (
        landed.reshape(panel_rows, OWN, BLK, BLK)
        .transpose(0, 2, 1, 3)
        .reshape(panel_rows * BLK, OWN * BLK)
    )
    target_col = panel_index * panel_rows * BLK + jnp.arange(panel_rows * BLK, dtype=jnp.int32)
    on_diagonal = jnp.arange(OWN * BLK, dtype=jnp.int32)[None, :] == target_col[:, None]
    assembled = assembled + jnp.where(on_diagonal, interface_diag[:, None], 0.0)
    row_ids = jnp.arange(panel_rows * BLK, dtype=jnp.int32)[:, None]
    position_ids = panel_index * panel_rows + row_ids // BLK
    column_part = jnp.where(position_ids != 0, interface_column, 0.0)
    assembled = jnp.concatenate([assembled[:, :BLK] + column_part, assembled[:, BLK:]], axis=1)
    own_column = assembled[:, :BLK]
    pivot_rows = jnp.logical_and(panel_index == 0, row_ids < BLK)
    whole_column = lax.all_gather(own_column, "panel", axis=0, tiled=True)
    pivot = jnp.linalg.cholesky(whole_column[:BLK])
    lower_all = lower_solve(pivot, whole_column)
    lower_all = jnp.concatenate([pivot, lower_all[BLK:]], axis=0)
    lower_own = lax.dynamic_slice_in_dim(
        lower_all, panel_index * panel_rows * BLK, panel_rows * BLK, 0
    )
    update = outer_product(lower_own, lower_all)
    updated = jnp.where(pivot_rows, assembled, assembled - update)
    factored = jnp.concatenate([lower_own, updated[:, BLK:]], axis=1)
    return (assembled, factored)


def solution(mesh):
    return jax.shard_map(
        per_device,
        mesh=mesh,
        in_specs=(
            P("sub", None, None),
            P("sub", None, "panel"),
            P(("sub", "panel")),
            P(("sub", "panel"), None),
            P(),
            P("sub", None),
        ),
        out_specs=(P(("sub", "panel"), None), P(("sub", "panel"), None)),
        check_vma=False,
    )
```

profile of v0, /device:TPU:8, one launch (start us, length us, event | category | flops | bytes accessed | tf_op | source)
XLA Modules:
  0.0 752.5 jit_solution(12533737966759849824)
XLA Ops:
  0.7 2.7 select_bitcast_fusion
  3.4 78.6 %custom-call.13 = f32[8,1,128,128]{2,3,1,0:T(8,128)S(1)} custom-call(f32[8,1,128,128]{3,2,1,0:T(8,128)S(1)} %get-tuple-element.19), custom_call_target="InvertDiagBlocksLowerTriangular" | custom-call | tf_op jit(solution)/shard_map/triangular_solve/custom-call.0 | solution.py:45
  82.0 6.5 copy.67
  88.5 1.0 fusion.35
  89.5 2.2 fusion.24
  91.7 5.8 fusion.37
  97.5 1.3 bitcast_dynamic-update-slice_fusion.3
  98.8 79.6 %custom-call.14 = f32[8,1,128,128]{2,3,1,0:T(8,128)S(1)} custom-call(f32[8,1,128,128]{3,2,1,0:T(8,128)} %get-tuple-element.18), custom_call_target="InvertDiagBlocksLowerTriangular" | custom-call | tf_op jit(solution)/shard_map/triangular_solve/custom-call.0 | solution.py:45
  178.3 1.0 fusion.33
  179.3 3.5 convert_element_type.50
  182.9 1.9 fusion.12
  184.8 10.2 %fusion.6 = f32[8,512,128]{2,1,0:T(8,128)} fusion(f32[8,128,512]{2,1,0:T(8,128)S(1)} %fusion.12, f32[8,128,512]{2,1,0:T(8,128)S(1)} %fusion.24, f32[8,512,512]{2,1,0:T(8,128)} %param.8), kind=kOutput, calls=%fused_computation.10 | convolution fusion | flops 1611661312 | bytes 7340032 | tf_op jit(solution)/shard_map/sik,skm->sim/dot_general | solution.py:53
  195.0 79.8 %custom-call.15 = f32[8,1,128,128]{2,3,1,0:T(8,128)S(1)} custom-call(f32[8,1,128,128]{3,2,1,0:T(8,128)} %get-tuple-element.17), custom_call_target="InvertDiagBlocksLowerTriangular" | custom-call | tf_op jit(solution)/shard_map/triangular_solve/custom-call.0 | solution.py:45
  274.8 1.0 fusion.31
  275.8 4.3 fusion.11
  280.2 14.1 %fusion = f32[8,512,128]{2,1,0:T(8,128)} fusion(f32[8,128,512]{2,1,0:T(8,128)S(1)} %fusion.11, f32[8,128,512]{2,1,0:T(8,128)S(1)} %copy-done.2, f32[8,128,512]{2,1,0:T(8,128)S(1)} %fusion.24, f32[8,512,512]{2,1,0:T(8,128)} %param.8), kind=kOutput, calls=%fused_computation.4 | convolution fusion | flops 2419064832 | bytes 9961472 | tf_op jit(solution)/shard_map/sik,skm->sim/dot_general | solution.py:53
  294.3 78.6 %custom-call.16 = f32[8,1,128,128]{2,3,1,0:T(8,128)S(1)} custom-call(f32[8,1,128,128]{3,2,1,0:T(8,128)S(1)} %get-tuple-element.16), custom_call_target="InvertDiagBlocksLowerTriangular" | custom-call | tf_op jit(solution)/shard_map/triangular_solve/custom-call.0 | solution.py:45
  372.9 1.0 fusion.29
  373.9 2.8 bitcast_dynamic-update-slice_fusion.2
  376.7 1.2 bitcast_dynamic-update-slice_fusion.1
  377.9 0.7 copy-done.6
  378.7 3.5 fusion.21
  382.1 1.3 bitcast_dynamic-update-slice_fusion
  383.4 1.7 constant_dynamic-slice_fusion
  385.2 2.6 copy.81
  387.8 3.0 collective-permute-start
  391.4 0.6 convert_reduce_fusion.2
  392.0 0.6 gather_fusion
  393.0 43.9 %collective-permute-done = bf16[8,512,256]{1,2,0:T(8,128)(2,1)S(1)} collective-permute-done((bf16[8,512,256]{1,2,0:T(8,128)(2,1)}, bf16[8,512,256]{1,2,0:T(8,128)(2,1)S(1)}, u32[]{:S(2)}, u32[]{:S(2)}) %collective-permute-start) | collective-permute-done | bytes 2097184 | tf_op jit(solution)/shard_map/ppermute | solution.py:13
  436.9 3.5 fusion.69
  440.4 3.0 collective-permute-start.1
  443.4 4.8 fusion.70
  448.2 1.6 copy.84
  449.8 5.2 collective-permute-done.1
  455.0 1.1 convert_bitcast_fusion
  456.2 1.5 maximum_select_fusion
  457.7 2.9 copy.88
  460.6 1.8 broadcast_multiply_fusion
  462.4 2.2 pad_maximum_fusion
  464.6 6.5 gather_fusion.1
  471.1 8.5 %select_multiply_fusion = f32[64,2,128,128]{3,2,1,0:T(8,128)} fusion(f32[64,2,128,128]{3,2,1,0:T(8,128)} %gather_fusion.1, f32[64]{0:T(128)S(1)} %convert_element_type.54, pred[64]{0:T(512)(128)(4,1)S(1)} %compare_and_fusion.2), kind=kLoop, calls=%fused_computation.3 | loop fusion | flops 4194304 | bytes 16777536 | tf_op jit(solution)/shard_map/mul | solution.py:114
  479.6 12.9 %all-to-all-start = ((f32[64,2,128,128]{3,2,1,0:T(8,128)}), f32[64,2,128,128]{3,2,1,0:T(8,128)}, u32[]{:S(2)}, u32[]{:S(2)}) async-start(f32[64,2,128,128]{3,2,1,0:T(8,128)} %select_multiply_fusion), calls=%async_computation | async-start | bytes 16777216 | tf_op jit(solution)/shard_map/all_to_all | solution.py:113
  493.2 0.5 copy.58
  493.7 0.5 eq.121
  494.5 0.2 convert_reduce_fusion
  494.8 1.0 copy.63
  495.8 0.5 eq.131
  496.6 0.3 broadcast_in_dim.86
  497.0 0.7 and.114
  497.8 0.7 fusion.22
  498.5 180.0 %all-to-all-done = f32[64,2,128,128]{3,2,1,0:T(8,128)} async-done(((f32[64,2,128,128]{3,2,1,0:T(8,128)}), f32[64,2,128,128]{3,2,1,0:T(8,128)}, u32[]{:S(2)}, u32[]{:S(2)}) %all-to-all-start) | async-done | bytes 8388640 | tf_op jit(solution)/shard_map/all_to_all | solution.py:113
  678.5 13.1 %copy.127 = f32[16,8,128,128]{3,1,2,0:T(8,128)} copy(f32[16,8,128,128]{3,2,1,0:T(8,128)} %bitcast.46) | data formatting | bytes 16777216
  691.7 9.0 %copy.89 = f32[128,16384]{0,1:T(8,128)} copy(f32[128,16384]{1,0:T(8,128)} %bitcast.121) | data formatting | bytes 16777216 | tf_op jit(solution)/shard_map/reshape | solution.py:141
  700.7 9.4 %fusion.71 = f32[2,8,128,128]{3,1,2,0:T(8,128)S(1)} fusion(f32[2,8,128,1]{2,1,3,0:T(8,128)S(1)} %fusion.22, f32[128,128,128,1]{2,1,0,3:T(8,128)} %bitcast.120), kind=kOutput, calls=%fused_computation.162 | convolution fusion | flops 402653184 | bytes 9445376 | tf_op jit(solution)/shard_map/dot_general | solution.py:139
  710.2 0.3 copy.114
  710.9 13.7 %all_gather.3 = f32[1024,128]{0,1:T(8,128)S(1)} all-gather(f32[256,128]{0,1:T(8,128)S(1)} %slice_add_fusion), channel_id=1, replica_groups=mesh['sub'=64,'panel'=4] {'panel'}, dimensions={0}, use_global_device_ids=true | all-gather | bytes 655360 | tf_op jit(solution)/shard_map/all_gather | solution.py:158
  724.8 11.7 %cholesky.14 = f32[128,128]{1,0:T(8,128)S(1)} custom-call(f32[128,128]{1,0:T(8,128)S(1)} %fusion.51), custom_call_target="Cholesky" | custom-call | tf_op jit(solution)/shard_map/jit(cholesky)/cholesky | solution.py:159
  736.5 0.6 compare_reduce_fusion
  737.2 0.7 select_bitcast_fusion.4
  737.9 9.8 %custom-call.9 = f32[1,128,128]{1,2,0:T(8,128)S(1)} custom-call(f32[1,128,128]{2,1,0:T(8,128)S(1)} %get-tuple-element.11), custom_call_target="InvertDiagBlocksLowerTriangular" | custom-call | tf_op jit(solution)/shard_map/triangular_solve | solution.py:30
  747.7 0.6 fusion.39
  748.4 1.0 fusion.28
  749.7 1.3 copy.97
  751.0 1.3 copy.96
  (74 shorter events, 3.6 us)
Async XLA Ops:
  179.3 3.5 copy-start.5
  182.8 12.2 %copy-start = (f32[8,512,512]{1,2,0:T(8,128)}, f32[8,512,512]{1,2,0:T(8,128)S(1)}, u32[]{:S(2)}) copy-start(f32[8,512,512]{1,2,0:T(8,128)S(1)} %convert_element_type.50) | copy-start | bytes 25165828
  184.8 10.3 %copy-start.1 = (f32[8,128,512]{2,1,0:T(8,128)}, f32[8,128,512]{2,1,0:T(8,128)S(1)}, u32[]{:S(2)}) copy-start(f32[8,128,512]{2,1,0:T(8,128)S(1)} %fusion.12) | copy-start | bytes 6291460
  275.8 4.3 copy-start.2
  280.1 14.1 %copy-start.3 = (f32[8,128,512]{2,1,0:T(8,128)}, f32[8,128,512]{2,1,0:T(8,128)S(1)}, u32[]{:S(2)}) copy-start(f32[8,128,512]{2,1,0:T(8,128)S(1)} %fusion.11) | copy-start | bytes 6291460
  372.9 3.8 copy-start.4
  376.7 2.0 copy-start.6
  385.2 5.7 copy-start.8
  385.2 6.1 copy-start.9
  387.8 49.1 %collective-permute-start = (bf16[8,512,256]{1,2,0:T(8,128)(2,1)}, bf16[8,512,256]{1,2,0:T(8,128)(2,1)S(1)}, u32[]{:S(2)}, u32[]{:S(2)}) collective-permute-start(bf16[8,512,256]{1,2,0:T(8,128)(2,1)} %bitcast.128), channel_id=1, source_target_pairs={{0,2},{1,3},{2,0},{3,1},{4,6},{5,7},{6,4},{7,5},{8,10},{9,11},{10,... | collective-permute-start | bytes 6291464 | tf_op jit(solution)/shard_map/ppermute | solution.py:13
  440.4 14.6 %collective-permute-start.1 = (bf16[8,2,128,128]{3,2,1,0:T(8,128)(2,1)}, bf16[8,2,128,128]{3,2,1,0:T(8,128)(2,1)}, u32[]{:S(2)}, u32[]{:S(2)}) collective-permute-start(bf16[8,2,128,128]{3,2,1,0:T(8,128)(2,1)} %get-tuple-element.26), channel_id=1, source_target_pairs={{0,2},{1,3},{2,0},{3,1},{4,6},{5,7},{6,4},{7,5},{8,10},{9,11},{10,... | collective-permute-start | bytes 1572872 | tf_op jit(solution)/shard_map/ppermute | solution.py:13
  479.6 198.9 %all-to-all-start = ((f32[64,2,128,128]{3,2,1,0:T(8,128)}), f32[64,2,128,128]{3,2,1,0:T(8,128)}, u32[]{:S(2)}, u32[]{:S(2)}) async-start(f32[64,2,128,128]{3,2,1,0:T(8,128)} %select_multiply_fusion), calls=%async_computation | async-start | bytes 16777216 | tf_op jit(solution)/shard_map/all_to_all | solution.py:113
  493.7 4.0 copy-start.7
  710.0 0.7 copy-start.10
where the time goes:
time: 761 us; the launch traced here: 752 us
  other arithmetic  368 us (48%)
  waiting for transfers between devices  229 us (30%)
  matrix products  65.9 us (9%)
  local copies, waits for them, and re-layouts  55.3 us (7%)
  starting transfers between devices  18.9 us (2%)
  blocking collectives  13.7 us (2%)
    another operation x6, other arithmetic, blocked_solve(): lax.linalg.triangular_solve(diag_block, identity, left_side=True, lower=T...  319 us
    all_to_all x1, waiting for transfers between devices, per_device(): lax.all_to_all(jnp.take(row_tiles, source, axis=0) * filled[:, None, None...  180 us
    ppermute x2, waiting for transfers between devices, partner(): return lax.ppermute(value, axis, pairs)  49.2 us
    dot_general x3, matrix products, blocked_solve(): jnp.einsum('sik,skm->sim', strip, earlier, precision=lax.Precision.HIGHEST)  30.2 us
    unnamed x29, local copies, waits for them, and re-layouts  23.5 us
  transfers between devices with their start and end apart: 3, of which 3 were waited for; matrix products, arithmetic and copies ran while one was open for 2% of the time, Pallas kernels for 0%

commit v1 on v0

v1 whole, which is shorter than its diff:
```python
import functools

import jax
import jax.numpy as jnp
from jax import lax
from jax.experimental import pallas as pl
from jax.experimental.pallas import tpu as pltpu
from jax.sharding import PartitionSpec as P

BLK = 128
HALF = BLK // 2
OWN = 8
BASE = 32
EXTRA = 8
F32 = jnp.float32
BF16 = jnp.bfloat16
VMEM = pltpu.VMEM


def split(x):
    hi = x.astype(BF16)
    return hi, (x - hi.astype(F32)).astype(BF16)


def mm(a, b):
    return jnp.dot(a, b, preferred_element_type=F32)


def mm_nt(a, b):
    return lax.dot_general(a, b, (((1,), (1,)), ((), ())), preferred_element_type=F32)


def mm_tn(a, b):
    return lax.dot_general(a, b, (((0,), (0,)), ((), ())), preferred_element_type=F32)


def wide(dot, a, b):
    ah, al = split(a)
    bh, bl = split(b)
    return dot(ah, bh) + (dot(ah, bl) + dot(al, bh))


def iota(shape, axis):
    return lax.broadcasted_iota(jnp.int32, shape, axis)


def base_inverses(f_ref, s_ref, a_ref, x_ref):
    subs, order, _ = f_ref.shape
    tiles = order // BLK
    per_tile = BLK // BASE
    count = subs * order // BASE

    def gather(l, carry):
        for t in range(tiles):
            for q in range(per_tile):
                row = t * BLK + q * BASE
                block = f_ref[l, row : row + BASE, t * BLK : (t + 1) * BLK]
                if q:
                    block = pltpu.roll(block, BLK - q * BASE, 1)
                s_ref[pl.ds(pl.multiple_of(l * order + row, BASE), BASE), :] = block
        return carry

    lax.fori_loop(0, subs, gather, 0)

    def lanes(i, carry):
        a_ref[i] = s_ref[pl.ds(i, count, stride=BASE), :].T[:BASE]
        return carry

    lax.fori_loop(0, BASE, lanes, 0, unroll=4)
    rows = iota((BASE, BLK), 0)
    for i in range(BASE):
        top = 8 * (i // 8 + 1)
        total = jnp.where(rows[:top] == i, 1.0, 0.0).astype(F32)
        parts = [total[8 * g : 8 * g + 8] for g in range(top // 8)]
        for k in range(i):
            factor = a_ref[i, k : k + 1, :]
            for g in range(k // 8 + 1):
                parts[g] = parts[g] - factor * x_ref[k, 8 * g : 8 * g + 8, :]
        scale = 1.0 / a_ref[i, i : i + 1, :]
        for g in range(BASE // 8):
            x_ref[i, 8 * g : 8 * g + 8, :] = (
                parts[g] * scale if g < len(parts) else jnp.zeros((8, BLK), F32)
            )

    def back(i, carry):
        padded = jnp.concatenate([x_ref[i], jnp.zeros((BLK - BASE, BLK), F32)], axis=0)
        s_ref[pl.ds(i, count, stride=BASE), :] = padded.T
        return carry

    lax.fori_loop(0, BASE, back, 0, unroll=4)


def full_inverse(l, f_ref, s_ref):
    order = f_ref.shape[1]
    tiles = order // BLK
    row = iota((BLK, BLK), 0)
    col = iota((BLK, BLK), 1)
    inverse = []
    for t in range(tiles):
        pieces = []
        for q in range(BLK // BASE):
            start = pl.multiple_of(l * order + t * BLK + q * BASE, BASE)
            block = s_ref[pl.ds(start, BASE), :]
            pieces.append(pltpu.roll(block, q * BASE, 1) if q else block)
        inverse.append(jnp.concatenate(pieces, axis=0))
    size = BASE
    while size < BLK:
        below = jnp.logical_and(row // size % 2 == 1, col // size == row // size - 1)
        for t in range(tiles):
            tile = f_ref[l, t * BLK : (t + 1) * BLK, t * BLK : (t + 1) * BLK]
            strip = wide(mm, jnp.where(below, tile, 0.0), inverse[t])
            inverse[t] = inverse[t] - wide(mm, inverse[t], strip)
        size *= 2
    while len(inverse) > 1:
        size = inverse[0].shape[0]
        merged = []
        for t in range(0, len(inverse), 2):
            below = f_ref[l, (t + 1) * size : (t + 2) * size, t * size : (t + 1) * size]
            corner = -wide(mm, inverse[t + 1], wide(mm, below, inverse[t]))
            if len(inverse) > 2:
                merged.append(
                    jnp.concatenate(
                        [
                            jnp.concatenate([inverse[t], jnp.zeros((size, size), F32)], axis=1),
                            jnp.concatenate([corner, inverse[t + 1]], axis=1),
                        ],
                        axis=0,
                    )
                )
            else:
                return inverse[0], corner, inverse[1]
        inverse = merged


def apply_inverse(hi_ref, lo_ref, right):
    half = hi_ref.shape[1] // 2
    top = mm(hi_ref[0, :half, :half], right[:half]) + mm(lo_ref[0, :half, :half], right[:half])
    low = mm(hi_ref[0, half:, :], right) + mm(lo_ref[0, half:, :], right)
    return jnp.concatenate([top.astype(BF16), low.astype(BF16)], axis=0)


def solve_kernel(slot_ref, upper_ref, f_ref, c_ref, hi_ref, lo_ref, w_ref, d_ref, s_ref, a_ref, x_ref):
    l = pl.program_id(0)
    order = f_ref.shape[1]
    half = order // 2
    groups = c_ref.shape[2] // BLK

    @pl.when(l == 0)
    def _():
        d_ref[...] = jnp.zeros_like(d_ref)
        base_inverses(f_ref, s_ref, a_ref, x_ref)

    left, corner, right = full_inverse(l, f_ref, s_ref)
    for part, rows, cols in ((left, 0, 0), (corner, half, 0), (right, half, half)):
        hi, lo = split(part)
        hi_ref[0, rows : rows + half, cols : cols + half] = hi
        lo_ref[0, rows : rows + half, cols : cols + half] = lo
    hi_ref[0, :half, half:] = jnp.zeros((half, half), BF16)
    lo_ref[0, :half, half:] = jnp.zeros((half, half), BF16)
    solved = apply_inverse(hi_ref, lo_ref, c_ref[0])
    width = solved.shape[1] // 2
    w_ref[0] = jnp.where(upper_ref[0] == 0, solved[:, :width], solved[:, width:])
    row = iota((HALF, BLK), 0)
    lane = iota((HALF, BLK), 1)
    from_low = lane - HALF < row
    eye = iota((BLK, BLK), 0) == iota((BLK, BLK), 1)
    extra_row = iota((EXTRA, BLK), 0)
    for r in range(groups):
        block = solved[:, r * BLK : (r + 1) * BLK]
        tile = mm_tn(block, block)
        folded = jnp.where(from_low, tile[HALF:], pltpu.roll(tile[:HALF], HALF, 1))
        diag = jnp.sum(jnp.where(eye, tile, 0.0), axis=0, keepdims=True)
        first = diag.astype(BF16).astype(F32)
        second = (diag - first).astype(BF16).astype(F32)
        third = diag - first - second
        extra = jnp.where(
            extra_row == 0,
            first,
            jnp.where(extra_row == 1, second, jnp.where(extra_row == 2, third, 0.0)),
        )
        slot = slot_ref[l * groups + r]
        d_ref[slot] = jnp.concatenate([folded, extra], axis=0).astype(BF16)


def cross_kernel(pat_ref, upper_ref, hi_ref, lo_ref, c_ref, w_ref, keep_ref, send_ref):
    l = pl.program_id(0)
    upper = upper_ref[0] == 0
    solved = apply_inverse(hi_ref, lo_ref, c_ref[0])
    for r in range(c_ref.shape[2] // BLK):
        own = w_ref[0, :, r * BLK : (r + 1) * BLK]
        other = solved[:, r * BLK : (r + 1) * BLK]
        tile = mm_tn(jnp.where(upper, own, other), jnp.where(upper, other, own))
        tile = tile * pat_ref[l * 2 + r].astype(F32)
        keep_ref[0, r] = jnp.where(upper, tile[:HALF], tile[HALF:]).astype(BF16)
        send_ref[0, r] = jnp.where(upper, tile[HALF:], tile[:HALF]).astype(BF16)


def place_kernel(slot_ref, keep_ref, got_ref, out_ref):
    out_ref[...] = jnp.zeros_like(out_ref)
    count = keep_ref.shape[0]

    def one(i, carry):
        out_ref[slot_ref[i]] = keep_ref[i]
        out_ref[slot_ref[count + i]] = got_ref[i]
        return carry

    lax.fori_loop(0, count, one, 0, unroll=2)


def diag_kernel(index_ref, recv_ref, own_diag_ref, out_ref, acc_ref):
    acc_ref[...] = jnp.zeros_like(acc_ref)

    def one(s, carry):
        i = index_ref[s]
        acc_ref[i] = acc_ref[i] + recv_ref[s].astype(F32)
        return carry

    lax.fori_loop(0, recv_ref.shape[0], one, 0, unroll=4)
    row = iota((HALF, BLK), 0)
    lane = iota((HALF, BLK), 1)
    eye = iota((BLK, BLK), 0) == iota((BLK, BLK), 1)
    for r in range(out_ref.shape[0]):
        folded = acc_ref[r + 1, :HALF, :]
        low = jnp.where(lane - HALF < row, folded, 0.0)
        high = jnp.where(
            jnp.logical_and(lane > row, lane < HALF), pltpu.roll(folded, HALF, 1), 0.0
        )
        strict = jnp.concatenate([high, low], axis=0)
        diag = jnp.sum(acc_ref[r + 1, HALF:, :], axis=0, keepdims=True) + own_diag_ref[r : r + 1, :]
        out_ref[r] = strict + strict.T + jnp.where(eye, diag, 0.0)


def cross_sum_kernel(index_ref, recv_ref, out_ref, acc_ref):
    acc_ref[...] = jnp.zeros_like(acc_ref)

    def one(s, carry):
        i = index_ref[s]
        acc_ref[i] = acc_ref[i] + recv_ref[s].astype(F32)
        return carry

    lax.fori_loop(0, recv_ref.shape[0], one, 0, unroll=4)
    out_ref[...] = acc_ref[1:]


def cholesky_kernel(tile_ref, p_ref, inv_ref, t_ref):
    groups = BLK // 8
    rows = [tile_ref[8 * g : 8 * g + 8, :] for g in range(groups)]
    lane = iota((8, BLK), 1)
    sub = iota((8, BLK), 0)
    lane1 = iota((1, BLK), 1)
    right = [jnp.where(lane == sub + 8 * g, 1.0, 0.0).astype(F32) for g in range(groups)]
    for j in range(BLK):
        g, s = divmod(j, 8)
        pivot_row = rows[g][s : s + 1, :]
        right_row = right[g][s : s + 1, :]
        pivot = jnp.broadcast_to(pivot_row[:, j : j + 1], (1, BLK))
        root = 1.0 / jnp.sqrt(pivot)
        scaled = pivot_row / pivot
        t_ref[j : j + 1, :] = jnp.where(lane1 >= j, pivot_row * root, 0.0)
        inv_ref[j : j + 1, :] = right_row * root
        right_scaled = right_row / pivot
        for h in range(g, groups):
            if h == g and s == 7:
                continue
            column = jnp.broadcast_to(rows[h][:, j : j + 1], (8, BLK))
            if h == g:
                column = jnp.where(sub > s, column, 0.0)
            rows[h] = rows[h] - column * scaled
            right[h] = right[h] - column * right_scaled
    p_ref[...] = t_ref[...].T


def final_kernel(panel_ref, diag_ref, half_ref, icol_ref, first_ref, p_ref, inv_ref, asm_ref, fac_ref, l_ref):
    panel = panel_ref[0]
    lower = panel < 2
    base = panel % 2
    other = (panel + 2) % 4
    asm_ref[...] = jnp.zeros_like(asm_ref)
    for r in range(2):
        at = pl.multiple_of((panel * 2 + r) * BLK, BLK)
        asm_ref[r * BLK : (r + 1) * BLK, pl.ds(at, BLK)] = diag_ref[r]
    for a in range(2):
        for b in range(2):
            whole = jnp.concatenate(
                [half_ref[base, a * 2 + b], half_ref[base + 2, a * 2 + b]], axis=0
            )
            tile = jnp.where(lower, whole, whole.T)
            row = pl.multiple_of(jnp.where(lower, a, b) * BLK, BLK)
            at = pl.multiple_of((other * 2 + jnp.where(lower, b, a)) * BLK, BLK)
            asm_ref[pl.ds(row, BLK), pl.ds(at, BLK)] = tile
    own = pl.multiple_of(panel * 2 * BLK, BLK)
    off = jnp.logical_or(panel > 0, iota((2 * BLK, BLK), 0) >= BLK)
    asm_ref[:, :BLK] = asm_ref[:, :BLK] + jnp.where(off, icol_ref[pl.ds(own, 2 * BLK), :], 0.0)
    inv_hi, inv_lo = split(inv_ref[...])
    l_ref[:BLK, :] = p_ref[...]
    for r in range(1, OWN):
        key = icol_ref[r * BLK : (r + 1) * BLK, :]
        if r in (4, 5):
            key = key + jnp.concatenate([half_ref[0, r - 4], half_ref[2, r - 4]], axis=0).T
        kh, kl = split(key)
        l_ref[r * BLK : (r + 1) * BLK, :] = mm_nt(kh, inv_hi) + (
            mm_nt(kh, inv_lo) + mm_nt(kl, inv_hi)
        )
    mine = l_ref[pl.ds(own, 2 * BLK), :]
    mh, ml = split(mine)
    fac_ref[:, :BLK] = mine
    for c in range(1, OWN):
        lh, ll = split(l_ref[c * BLK : (c + 1) * BLK, :])
        update = mm_nt(mh, lh) + (mm_nt(mh, ll) + mm_nt(ml, lh))
        fac_ref[:, c * BLK : (c + 1) * BLK] = asm_ref[:, c * BLK : (c + 1) * BLK] - jnp.where(
            off, update, 0.0
        )


def cost(flops, nbytes):
    return pl.CostEstimate(flops=flops, bytes_accessed=nbytes, transcendentals=0)


def whole(count):
    return [pl.BlockSpec(memory_space=VMEM)] * count


SMEM = pl.BlockSpec(memory_space=pltpu.SMEM)


def partner(value, panels):
    pairs = [(source, (source + panels // 2) % panels) for source in range(panels)]
    return lax.ppermute(value, "panel", pairs)


def per_device(
    interior_factor, coupling, interface_diag, interface_column, block_map, pair_pattern
):
    subs, order, width = coupling.shape
    owners_total = lax.axis_size("sub")
    panels = lax.axis_size("panel")
    sub = lax.axis_index("sub")
    panel = lax.axis_index("panel")
    upper = (panel >= panels // 2).astype(jnp.int32)
    upper_s = upper.reshape(1)
    panel_s = panel.astype(jnp.int32).reshape(1)
    groups = width // BLK
    half_width = width // 2

    outgoing = lax.dynamic_slice_in_dim(coupling, (1 - upper) * half_width, half_width, 2)
    incoming = partner(outgoing, panels)
    columns = lax.all_gather(interface_column, "panel", axis=0, tiled=True)

    maps = block_map.reshape(owners_total, subs, panels, groups)
    owner = maps[:, :, 0, :] // OWN
    match = (owner == sub).astype(jnp.int32)
    place = maps % 2
    base = panel % 2
    own_place = lax.dynamic_index_in_dim(place, panel, 2, keepdims=False)
    low_place = lax.dynamic_index_in_dim(place, base, 2, keepdims=False)
    high_place = lax.dynamic_index_in_dim(place, base + 2, 2, keepdims=False)
    diag_index = jnp.sum(match * (1 + own_place), axis=(1, 2))
    cross_index = jnp.sum(match * (1 + 2 * low_place + high_place), axis=(1, 2))
    slots = lax.dynamic_index_in_dim(owner, sub, 0, keepdims=False)
    by_half = slots.reshape(subs, 2, 2)
    keep_slots = lax.dynamic_index_in_dim(by_half, upper, 1, keepdims=False).reshape(-1)
    got_slots = lax.dynamic_index_in_dim(by_half, 1 - upper, 1, keepdims=False).reshape(-1)
    pattern = lax.dynamic_slice_in_dim(pair_pattern, base * groups + upper * 2, 2, 1).reshape(-1)

    hi, lo, w_half, diag_send = pl.pallas_call(
        solve_kernel,
        grid=(subs,),
        in_specs=[
            SMEM,
            SMEM,
            pl.BlockSpec((subs, order, order), lambda l: (0, 0, 0)),
            pl.BlockSpec((1, order, width), lambda l: (l, 0, 0)),
        ],
        out_specs=[
            pl.BlockSpec((1, order, order), lambda l: (l, 0, 0)),
            pl.BlockSpec((1, order, order), lambda l: (l, 0, 0)),
            pl.BlockSpec((1, order, half_width), lambda l: (l, 0, 0)),
            pl.BlockSpec((owners_total, HALF + EXTRA, BLK), lambda l: (0, 0, 0)),
        ],
        out_shape=[
            jax.ShapeDtypeStruct((subs, order, order), BF16),
            jax.ShapeDtypeStruct((subs, order, order), BF16),
            jax.ShapeDtypeStruct((subs, order, half_width), BF16),
            jax.ShapeDtypeStruct((owners_total, HALF + EXTRA, BLK), BF16),
        ],
        scratch_shapes=[
            VMEM((subs * order, BLK), F32),
            VMEM((BASE, BASE, BLK), F32),
            VMEM((BASE, BASE, BLK), F32),
        ],
        compiler_params=pltpu.CompilerParams(vmem_limit_bytes=48 * 2**20),
        cost_estimate=cost(2 * 10**10, 2**25),
        name="solve",
    )(slots.reshape(-1), upper_s, interior_factor, coupling)

    diag_got = lax.all_to_all(diag_send, "sub", split_axis=0, concat_axis=0, tiled=True)

    keep, send = pl.pallas_call(
        cross_kernel,
        grid=(subs,),
        in_specs=[
            SMEM,
            SMEM,
            pl.BlockSpec((1, order, order), lambda l: (l, 0, 0)),
            pl.BlockSpec((1, order, order), lambda l: (l, 0, 0)),
            pl.BlockSpec((1, order, half_width), lambda l: (l, 0, 0)),
            pl.BlockSpec((1, order, half_width), lambda l: (l, 0, 0)),
        ],
        out_specs=[pl.BlockSpec((1, 2, HALF, BLK), lambda l: (l, 0, 0, 0))] * 2,
        out_shape=[jax.ShapeDtypeStruct((subs, 2, HALF, BLK), BF16)] * 2,
        cost_estimate=cost(4 * 10**9, 2**24),
        name="cross",
    )(pattern, upper_s, hi, lo, incoming, w_half)
    got = partner(send, panels)

    count = subs * 2
    cross_send = pl.pallas_call(
        place_kernel,
        in_specs=[SMEM] + whole(2),
        out_specs=pl.BlockSpec(memory_space=VMEM),
        out_shape=jax.ShapeDtypeStruct((owners_total, HALF, BLK), BF16),
        cost_estimate=cost(10**9, 2**21),
        name="place",
    )(
        jnp.concatenate([keep_slots, got_slots]),
        keep.reshape(count, HALF, BLK),
        got.reshape(count, HALF, BLK),
    )
    cross_got = lax.all_to_all(cross_send, "sub", split_axis=0, concat_axis=0, tiled=True)

    rows = OWN // panels
    diag_tiles = pl.pallas_call(
        diag_kernel,
        in_specs=[SMEM] + whole(2),
        out_specs=pl.BlockSpec(memory_space=VMEM),
        out_shape=jax.ShapeDtypeStruct((rows, BLK, BLK), F32),
        scratch_shapes=[VMEM((rows + 1, HALF + EXTRA, BLK), F32)],
        cost_estimate=cost(10**9, 2**21),
        name="diag_sum",
    )(diag_index, diag_got, interface_diag.reshape(rows, BLK))
    first = lax.all_gather(diag_tiles[0], "panel", axis=0)[0]
    pivot, pivot_inverse = pl.pallas_call(
        cholesky_kernel,
        in_specs=whole(1),
        out_specs=whole(2),
        out_shape=[jax.ShapeDtypeStruct((BLK, BLK), F32)] * 2,
        scratch_shapes=[VMEM((BLK, BLK), F32)],
        cost_estimate=cost(10**10, 2**18),
        name="pivot",
    )(first)

    halves = pl.pallas_call(
        cross_sum_kernel,
        in_specs=[SMEM] + whole(1),
        out_specs=pl.BlockSpec(memory_space=VMEM),
        out_shape=jax.ShapeDtypeStruct((rows * rows, HALF, BLK), F32),
        scratch_shapes=[VMEM((rows * rows + 1, HALF, BLK), F32)],
        cost_estimate=cost(10**9, 2**21),
        name="cross_sum",
    )(cross_index, cross_got)
    all_halves = lax.all_gather(halves, "panel", axis=0)
    return pl.pallas_call(
        final_kernel,
        in_specs=[SMEM] + whole(6),
        out_specs=whole(2),
        out_shape=[jax.ShapeDtypeStruct((rows * BLK, OWN * BLK), F32)] * 2,
        scratch_shapes=[VMEM((OWN * BLK, BLK), F32)],
        cost_estimate=cost(10**9, 2**22),
        name="final",
    )(panel_s, diag_tiles, all_halves, columns, first, pivot, pivot_inverse)


def solution(mesh):
    return jax.shard_map(
        per_device,
        mesh=mesh,
        in_specs=(
            P("sub", None, None),
            P("sub", None, "panel"),
            P(("sub", "panel")),
            P(("sub", "panel"), None),
            P(),
            P("sub", None),
        ),
        out_specs=(P(("sub", "panel"), None), P(("sub", "panel"), None)),
        check_vma=False,
    )
```

time: 761 us -> 151 us (0.20); the launches traced: 752 us -> 151 us
  other arithmetic: 368 us -> 1.64 us
  waiting for transfers between devices: 229 us -> 13.8 us
  matrix products: 65.9 us -> 0 us
  Pallas kernels: 0 us -> 62.9 us
  local copies, waits for them, and re-layouts: 55.3 us -> 7.72 us
  blocking collectives: 13.7 us -> 39.9 us
    another operation x15 -> x0, other arithmetic: 345 us -> none  [the longest x6 319 us: blocked_solve(): lax.linalg.triangular_solve(diag_block, identity, left_side=True, lower=T...]
    all_to_all x1 -> x2, waiting for transfers between devices: 180 us -> 7.66 us  [the longest x1 7.66 us: per_device(): lax.all_to_all(diag_send, 'sub', split_axis=0, concat_axis=0, tiled=True)]
    pallas_call x0 -> x7, Pallas kernels: none -> 62.9 us  [the longest x1 29.8 us: per_device(): pl.pallas_call(solve_kernel, grid=(subs,), in_specs=[SMEM, SMEM, pl.Block...]
    dot_general x12 -> x0, matrix products: 61.4 us -> none  [the longest x3 30.2 us: blocked_solve(): jnp.einsum('sik,skm->sim', strip, earlier, precision=lax.Precision.HIGHEST)]
    ppermute x2, waiting for transfers between devices: 49.2 us -> 6.11 us  [partner(): return lax.ppermute(value, 'panel', pairs)]
    all_gather x1 -> x3, blocking collectives: 13.7 us -> 39.9 us  [the longest x1 14 us: per_device(): all_halves = lax.all_gather(halves, 'panel', axis=0)]
    unnamed x29 -> x12, local copies, waits for them, and re-layouts: 23.5 us -> 3 us
    mul x3 -> x0, other arithmetic: 10.3 us -> none  [the longest x1 8.54 us: per_device(): jnp.take(row_tiles, source, axis=0) * filled[:, None, None, None]]
  transfers between devices with their start and end apart: 3 -> 4, of which waited for: 3 -> 3; matrix products, arithmetic and copies ran while one was open for 2% -> 3% of each run, Pallas kernels for 0% -> 38%
where the time goes in v1:
time: 151 us
  Pallas kernels  62.9 us (42%)
  blocking collectives  39.9 us (26%)
  starting transfers between devices  24.1 us (16%)
  waiting for transfers between devices  13.8 us (9%)
  local copies, waits for them, and re-layouts  7.72 us (5%)
  other arithmetic  1.64 us (1%)
    pallas_call x1, Pallas kernels, per_device(): pl.pallas_call(solve_kernel, grid=(subs,), in_specs=[SMEM, SMEM, pl.Block...  29.8 us
    all_gather x1, blocking collectives, per_device(): all_halves = lax.all_gather(halves, 'panel', axis=0)  14 us
    all_gather x1, blocking collectives, per_device(): columns = lax.all_gather(interface_column, 'panel', axis=0, tiled=True)  13.5 us
    all_gather x1, blocking collectives, per_device(): first = lax.all_gather(diag_tiles[0], 'panel', axis=0)[0]  12.4 us
    all_to_all x1, starting transfers between devices, per_device(): lax.all_to_all(diag_send, 'sub', split_axis=0, concat_axis=0, tiled=True)  12.3 us
    pallas_call x1, Pallas kernels, per_device(): pl.pallas_call(cholesky_kernel, in_specs=whole(1), out_specs=whole(2), ou...  12.2 us
    pallas_call x1, Pallas kernels, per_device(): pl.pallas_call(cross_kernel, grid=(subs,), in_specs=[SMEM, SMEM, pl.Block...  10.1 us
    all_to_all x1, waiting for transfers between devices, per_device(): lax.all_to_all(diag_send, 'sub', split_axis=0, concat_axis=0, tiled=True)  7.66 us
  transfers between devices with their start and end apart: 4, of which 3 were waited for; matrix products, arithmetic and copies ran while one was open for 3% of the time, Pallas kernels for 38%

profile of v1, /device:TPU:8, one launch (start us, length us, event | category | flops | bytes accessed | tf_op | source)
XLA Modules:
  0.0 150.8 jit_solution(1703011521885176684)
XLA Ops:
  0.6 0.0 copy-start
  0.7 0.0 copy-start.4
  0.7 1.7 %constant_dynamic-slice_fusion.4 = bf16[8,512,256]{2,1,0:T(8,128)(2,1)S(1)} fusion(bf16[8,512,512]{2,1,0:T(8,128)(2,1)} %c_ref.1, s32[]{:T(128)S(6)} %select_n.55), kind=kLoop, calls=%fused_computation.22 | loop fusion | bytes 4194308 | tf_op jit(solution)/shard_map/dynamic_slice | solution.py:345
  2.4 3.1 %collective-permute-start = (bf16[8,512,256]{2,1,0:T(8,128)(2,1)S(1)}, bf16[8,512,256]{2,1,0:T(8,128)(2,1)}, u32[]{:S(2)}, u32[]{:S(2)}) collective-permute-start(bf16[8,512,256]{2,1,0:T(8,128)(2,1)S(1)} %constant_dynamic-slice_fusion.4), channel_id=1, source_target_pairs={{0,2},{1,3},{2,0},{3,1},{4,6},{5,7},{6,4},{7,5},{8,10},{9,11},{10,... | collective-permute-start | bytes 6291464 | tf_op jit(solution)/shard_map/ppermute | solution.py:328
  5.5 0.0 copy-done.4
  5.5 0.3 reshape.49
  5.8 0.1 broadcast_compare_fusion
  6.0 0.1 copy.18
  6.0 0.1 reshape.50.slot_ref
  6.1 29.8 %solve.1 = (bf16[8,512,512]{2,1,0:T(8,128)(2,1)}, bf16[8,512,512]{2,1,0:T(8,128)(2,1)}, bf16[8,512,256]{2,1,0:T(8,128)(2,1)S(1)}, bf16[64,72,128]{2,1,0:T(8,128)(2,1)}) custom-call(s32[32]{0:T(128)S(1)} %reshape.50.slot_ref, s32[1]{0:T(128)} %bitcast.3.upper_ref, f32[8,512,512]{2,1,0:T(8,128)} %f_ref.1, bf16[8,512,512]{2,1,0:T(8,128)(2,1)} %c_ref.1), custom_call_target="tpu_custom_call" | custom-call | flops 20000000000 | bytes 33554432 | tf_op jit(solution)/shard_map/solve/pallas_call | solution.py:365
  35.9 0.0 copy-start.1
  35.9 1.3 copy-done.1
  37.2 12.3 %all-to-all-start = ((bf16[64,72,128]{2,1,0:T(8,128)(2,1)}), bf16[64,72,128]{2,1,0:T(8,128)(2,1)}, u32[]{:S(2)}, u32[]{:S(2)}) async-start(bf16[64,72,128]{2,1,0:T(8,128)(2,1)} %get-tuple-element.10), calls=%async_computation | async-start | bytes 2359296 | tf_op jit(solution)/shard_map/all_to_all | solution.py:396
  49.5 0.0 copy-done
  49.5 0.1 constant_dynamic-slice_fusion
  49.6 0.6 reshape.56.pat_ref
  50.2 1.2 collective-permute-done.c_ref
  51.5 10.1 %cross.1 = (bf16[8,2,64,128]{3,2,1,0:T(8,128)(2,1)}, bf16[8,2,64,128]{3,2,1,0:T(8,128)(2,1)}) custom-call(s32[16]{0:T(128)} %reshape.56.pat_ref, s32[1]{0:T(128)} %bitcast.3.upper_ref, bf16[8,512,512]{2,1,0:T(8,128)(2,1)} %get-tuple-element.11.hi_ref, bf16[8,512,512]{2,1,0:T(8,128)(2,1)} %get-tuple-element.12.lo_ref, ...), custom_call_target="tpu_custom_call" | custom-call | flops 4000000000 | bytes 16777216 | tf_op jit(solution)/shard_map/cross/pallas_call | solution.py:398
  61.5 3.0 %collective-permute-start.1 = (bf16[8,2,64,128]{3,2,1,0:T(8,128)(2,1)}, bf16[8,2,64,128]{3,2,1,0:T(8,128)(2,1)S(1)}, u32[]{:S(2)}, u32[]{:S(2)}) collective-permute-start(bf16[8,2,64,128]{3,2,1,0:T(8,128)(2,1)} %get-tuple-element.15), channel_id=1, source_target_pairs={{0,2},{1,3},{2,0},{3,1},{4,6},{5,7},{6,4},{7,5},{8,10},{9,11},{10,... | collective-permute-start | bytes 786440 | tf_op jit(solution)/shard_map/ppermute | solution.py:328
  64.6 0.1 copy.19
  64.6 0.1 reshape.54
  64.7 0.1 copy.20
  64.8 0.1 reshape.55
  64.9 0.7 pad_add_fusion.slot_ref
  65.6 4.9 %collective-permute-done.1 = bf16[8,2,64,128]{3,2,1,0:T(8,128)(2,1)S(1)} collective-permute-done((bf16[8,2,64,128]{3,2,1,0:T(8,128)(2,1)}, bf16[8,2,64,128]{3,2,1,0:T(8,128)(2,1)S(1)}, u32[]{:S(2)}, u32[]{:S(2)}) %collective-permute-start.1) | collective-permute-done | bytes 262176 | tf_op jit(solution)/shard_map/ppermute | solution.py:328
  70.4 0.0 copy-start.5
  70.4 0.7 copy-done.5
  71.1 2.2 %place.1 = bf16[64,64,128]{2,1,0:T(8,128)(2,1)} custom-call(s32[32]{0:T(128)} %pad_add_fusion.slot_ref, bf16[16,64,128]{2,1,0:T(8,128)(2,1)} %bitcast.32, bf16[16,64,128]{2,1,0:T(8,128)(2,1)} %bitcast.30), custom_call_target="tpu_custom_call" | custom-call | flops 1000000000 | bytes 2097152 | tf_op jit(solution)/shard_map/place/pallas_call | solution.py:417
  73.4 0.0 copy-start.3
  73.4 7.7 %all-to-all-done.recv_ref = bf16[64,72,128]{2,1,0:T(8,128)(2,1)} async-done(((bf16[64,72,128]{2,1,0:T(8,128)(2,1)}), bf16[64,72,128]{2,1,0:T(8,128)(2,1)}, u32[]{:S(2)}, u32[]{:S(2)}) %all-to-all-start) | async-done | bytes 1179680 | tf_op jit(solution)/shard_map/all_to_all | solution.py:396
  81.0 5.6 %all-to-all-start.1 = ((bf16[64,64,128]{2,1,0:T(8,128)(2,1)}), bf16[64,64,128]{2,1,0:T(8,128)(2,1)S(1)}, u32[]{:S(2)}, u32[]{:S(2)}) async-start(bf16[64,64,128]{2,1,0:T(8,128)(2,1)} %place.1), calls=%async_computation.1 | async-start | bytes 2097152 | tf_op jit(solution)/shard_map/all_to_all | solution.py:429
  86.7 0.2 add_select_fusion
  86.9 0.7 fusion.2
  87.6 0.0 copy-done.3
  87.6 13.5 %all_gather.14.icol_ref = f32[1024,128]{1,0:T(8,128)} all-gather(f32[256,128]{1,0:T(8,128)S(1)} %copy-done.3), channel_id=1, replica_groups=mesh['sub'=64,'panel'=4] {'panel'}, dimensions={0}, use_global_device_ids=true | all-gather | bytes 655360 | tf_op jit(solution)/shard_map/all_gather | solution.py:347
  101.1 2.5 %diag_sum.1.diag_ref = f32[2,128,128]{2,1,0:T(8,128)} custom-call(s32[64]{0:T(128)} %get-tuple-element.19.index_ref, bf16[64,72,128]{2,1,0:T(8,128)(2,1)} %all-to-all-done.recv_ref, f32[2,128]{1,0:T(2,128)} %bitcast.31), custom_call_target="tpu_custom_call" | custom-call | flops 1000000000 | bytes 2097152 | tf_op jit(solution)/shard_map/diag_sum/pallas_call | solution.py:432
  103.6 0.8 slice.13
  104.5 12.4 %all_gather.15 = f32[4,128,128]{2,1,0:T(8,128)S(1)} all-gather(f32[1,128,128]{2,1,0:T(8,128)S(1)} %slice.13), channel_id=1, replica_groups=mesh['sub'=64,'panel'=4] {'panel'}, dimensions={0}, use_global_device_ids=true | all-gather | bytes 327680 | tf_op jit(solution)/shard_map/all_gather | solution.py:441
  116.9 0.6 slice_bitcast_fusion.1.tile_ref.first_ref
  117.5 12.2 %pivot.1 = (f32[128,128]{1,0:T(8,128)}, f32[128,128]{1,0:T(8,128)}) custom-call(f32[128,128]{1,0:T(8,128)} %slice_bitcast_fusion.1.tile_ref.first_ref), custom_call_target="tpu_custom_call" | custom-call | flops 10000000000 | bytes 262144 | tf_op jit(solution)/shard_map/pivot/pallas_call | solution.py:442
  129.8 0.0 all-to-all-done.1.recv_ref
  129.8 0.0 copy-start.2
  129.8 1.0 copy-done.2
  130.7 2.3 %cross_sum.1 = f32[4,64,128]{2,1,0:T(8,128)} custom-call(s32[64]{0:T(128)} %get-tuple-element.18.index_ref, bf16[64,64,128]{2,1,0:T(8,128)(2,1)} %copy-done.2), custom_call_target="tpu_custom_call" | custom-call | flops 1000000000 | bytes 2097152 | tf_op jit(solution)/shard_map/cross_sum/pallas_call | solution.py:452
  133.0 14.0 %all-gather = f32[16,64,128]{2,1,0:T(8,128)} all-gather(f32[4,64,128]{2,1,0:T(8,128)} %cross_sum.1), channel_id=2, replica_groups=mesh['sub'=64,'panel'=4] {'panel'}, dimensions={0}, use_global_device_ids=true | all-gather | bytes 655360 | tf_op jit(solution)/shard_map/all_gather | solution.py:461
  147.0 3.8 %final.1 = (f32[256,1024]{1,0:T(8,128)}, f32[256,1024]{1,0:T(8,128)}) custom-call(s32[1]{0:T(128)} %bitcast.panel_ref, f32[2,128,128]{2,1,0:T(8,128)} %diag_sum.1.diag_ref, f32[4,4,64,128]{3,2,1,0:T(8,128)} %bitcast.28, f32[1024,128]{1,0:T(8,128)} %all_gather.14.icol_ref, f32[128,128]{1,0:T(8,128)} %slice_bitcast_fusion.1.tile_ref.first_ref, ...), custom_call_target="tpu_custom_call" | custom-call | flops 1000000000 | bytes 4194304 | tf_op jit(solution)/shard_map/final/pallas_call | solution.py:462
  (2 shorter events, 0.0 us)
Async XLA Ops:
  0.6 48.9 %copy-start = (s32[8,8]{1,0:T(8,128)S(1)}, s32[8,8]{1,0:T(8,128)}, u32[]{:S(2)}) copy-start(s32[8,8]{1,0:T(8,128)} %param.11) | copy-start | bytes 772
  0.7 4.9 %copy-start.4 = (s32[512,16]{0,1:T(8,128)S(1)}, s32[512,16]{0,1:T(8,128)}, u32[]{:S(2)}) copy-start(s32[512,16]{0,1:T(8,128)} %param.10) | copy-start | bytes 98308
  2.4 49.1 %collective-permute-start = (bf16[8,512,256]{2,1,0:T(8,128)(2,1)S(1)}, bf16[8,512,256]{2,1,0:T(8,128)(2,1)}, u32[]{:S(2)}, u32[]{:S(2)}) collective-permute-start(bf16[8,512,256]{2,1,0:T(8,128)(2,1)S(1)} %constant_dynamic-slice_fusion.4), channel_id=1, source_target_pairs={{0,2},{1,3},{2,0},{3,1},{4,6},{5,7},{6,4},{7,5},{8,10},{9,11},{10,... | collective-permute-start | bytes 6291464 | tf_op jit(solution)/shard_map/ppermute | solution.py:328
  35.9 1.3 copy-start.1
  37.2 43.8 %all-to-all-start = ((bf16[64,72,128]{2,1,0:T(8,128)(2,1)}), bf16[64,72,128]{2,1,0:T(8,128)(2,1)}, u32[]{:S(2)}, u32[]{:S(2)}) async-start(bf16[64,72,128]{2,1,0:T(8,128)(2,1)} %get-tuple-element.10), calls=%async_computation | async-start | bytes 2359296 | tf_op jit(solution)/shard_map/all_to_all | solution.py:396
  61.5 8.9 %collective-permute-start.1 = (bf16[8,2,64,128]{3,2,1,0:T(8,128)(2,1)}, bf16[8,2,64,128]{3,2,1,0:T(8,128)(2,1)S(1)}, u32[]{:S(2)}, u32[]{:S(2)}) collective-permute-start(bf16[8,2,64,128]{3,2,1,0:T(8,128)(2,1)} %get-tuple-element.15), channel_id=1, source_target_pairs={{0,2},{1,3},{2,0},{3,1},{4,6},{5,7},{6,4},{7,5},{8,10},{9,11},{10,... | collective-permute-start | bytes 786440 | tf_op jit(solution)/shard_map/ppermute | solution.py:328
  70.4 0.7 copy-start.5
  73.4 14.2 %copy-start.3 = (f32[256,128]{1,0:T(8,128)S(1)}, f32[256,128]{1,0:T(8,128)}, u32[]{:S(2)}) copy-start(f32[256,128]{1,0:T(8,128)} %param.9) | copy-start | bytes 393220
  81.0 48.8 %all-to-all-start.1 = ((bf16[64,64,128]{2,1,0:T(8,128)(2,1)}), bf16[64,64,128]{2,1,0:T(8,128)(2,1)S(1)}, u32[]{:S(2)}, u32[]{:S(2)}) async-start(bf16[64,64,128]{2,1,0:T(8,128)(2,1)} %place.1), calls=%async_computation.1 | async-start | bytes 2097152 | tf_op jit(solution)/shard_map/all_to_all | solution.py:429
  129.8 1.0 copy-start.2

commit v2 on v1

v2 whole, which is shorter than its diff:
```python
import functools

import jax
import jax.numpy as jnp
from jax import lax
from jax.experimental import pallas as pl
from jax.experimental.pallas import tpu as pltpu
from jax.sharding import PartitionSpec as P

BLK = 128
HALF = BLK // 2
OWN = 8
BASE = 32
EXTRA = 8
EARLY = 5
F32 = jnp.float32
BF16 = jnp.bfloat16
VMEM = pltpu.VMEM


def split(x):
    hi = x.astype(BF16)
    return hi, (x - hi.astype(F32)).astype(BF16)


def mm(a, b):
    return jnp.dot(a, b, preferred_element_type=F32)


def mm_nt(a, b):
    return lax.dot_general(a, b, (((1,), (1,)), ((), ())), preferred_element_type=F32)


def mm_tn(a, b):
    return lax.dot_general(a, b, (((0,), (0,)), ((), ())), preferred_element_type=F32)


def wide(dot, a, b):
    ah, al = split(a)
    bh, bl = split(b)
    return dot(ah, bh) + (dot(ah, bl) + dot(al, bh))


def iota(shape, axis):
    return lax.broadcasted_iota(jnp.int32, shape, axis)


def base_inverses(f_ref, s_ref, a_ref, x_ref):
    subs, order, _ = f_ref.shape
    tiles = order // BLK
    per_tile = BLK // BASE
    count = subs * order // BASE

    def gather(l, carry):
        for t in range(tiles):
            for q in range(per_tile):
                row = t * BLK + q * BASE
                block = f_ref[l, row : row + BASE, t * BLK : (t + 1) * BLK]
                if q:
                    block = pltpu.roll(block, BLK - q * BASE, 1)
                s_ref[pl.ds(pl.multiple_of(l * order + row, BASE), BASE), :] = block
        return carry

    lax.fori_loop(0, subs, gather, 0)

    def lanes(i, carry):
        a_ref[i] = s_ref[pl.ds(i, count, stride=BASE), :].T[:BASE]
        return carry

    lax.fori_loop(0, BASE, lanes, 0, unroll=4)
    rows = iota((BASE, BLK), 0)
    for i in range(BASE):
        top = 8 * (i // 8 + 1)
        total = jnp.where(rows[:top] == i, 1.0, 0.0).astype(F32)
        parts = [total[8 * g : 8 * g + 8] for g in range(top // 8)]
        for k in range(i):
            factor = a_ref[i, k : k + 1, :]
            for g in range(k // 8 + 1):
                parts[g] = parts[g] - factor * x_ref[k, 8 * g : 8 * g + 8, :]
        scale = 1.0 / a_ref[i, i : i + 1, :]
        for g in range(BASE // 8):
            x_ref[i, 8 * g : 8 * g + 8, :] = (
                parts[g] * scale if g < len(parts) else jnp.zeros((8, BLK), F32)
            )

    def back(i, carry):
        padded = jnp.concatenate([x_ref[i], jnp.zeros((BLK - BASE, BLK), F32)], axis=0)
        s_ref[pl.ds(i, count, stride=BASE), :] = padded.T
        return carry

    lax.fori_loop(0, BASE, back, 0, unroll=4)


def full_inverse(l, f_ref, s_ref):
    order = f_ref.shape[1]
    tiles = order // BLK
    row = iota((BLK, BLK), 0)
    col = iota((BLK, BLK), 1)
    inverse = []
    for t in range(tiles):
        pieces = []
        for q in range(BLK // BASE):
            start = pl.multiple_of(l * order + t * BLK + q * BASE, BASE)
            block = s_ref[pl.ds(start, BASE), :]
            pieces.append(pltpu.roll(block, q * BASE, 1) if q else block)
        inverse.append(jnp.concatenate(pieces, axis=0))
    size = BASE
    while size < BLK:
        below = jnp.logical_and(row // size % 2 == 1, col // size == row // size - 1)
        for t in range(tiles):
            tile = f_ref[l, t * BLK : (t + 1) * BLK, t * BLK : (t + 1) * BLK]
            strip = wide(mm, jnp.where(below, tile, 0.0), inverse[t])
            inverse[t] = inverse[t] - wide(mm, inverse[t], strip)
        size *= 2
    while len(inverse) > 1:
        size = inverse[0].shape[0]
        merged = []
        for t in range(0, len(inverse), 2):
            below = f_ref[l, (t + 1) * size : (t + 2) * size, t * size : (t + 1) * size]
            corner = -wide(mm, inverse[t + 1], wide(mm, below, inverse[t]))
            if len(inverse) > 2:
                merged.append(
                    jnp.concatenate(
                        [
                            jnp.concatenate([inverse[t], jnp.zeros((size, size), F32)], axis=1),
                            jnp.concatenate([corner, inverse[t + 1]], axis=1),
                        ],
                        axis=0,
                    )
                )
            else:
                return inverse[0], corner, inverse[1]
        inverse = merged


def apply_inverse(hi, lo, right):
    half = hi.shape[0] // 2
    top = mm(hi[:half, :half], right[:half]) + mm(lo[:half, :half], right[:half])
    low = mm(hi[half:], right) + mm(lo[half:], right)
    return jnp.concatenate([top.astype(BF16), low.astype(BF16)], axis=0)


def solve_kernel(upper_ref, f_ref, c_ref, hi_ref, lo_ref, w_ref, d_ref, s_ref, a_ref, x_ref):
    l = pl.program_id(0)
    order = f_ref.shape[1]
    half = order // 2
    groups = c_ref.shape[2] // BLK

    @pl.when(l == 0)
    def _():
        d_ref[...] = jnp.zeros_like(d_ref)
        base_inverses(f_ref, s_ref, a_ref, x_ref)

    left, corner, right = full_inverse(l, f_ref, s_ref)
    for part, rows, cols in ((left, 0, 0), (corner, half, 0), (right, half, half)):
        hi, lo = split(part)
        hi_ref[0, rows : rows + half, cols : cols + half] = hi
        lo_ref[0, rows : rows + half, cols : cols + half] = lo
    hi_ref[0, :half, half:] = jnp.zeros((half, half), BF16)
    lo_ref[0, :half, half:] = jnp.zeros((half, half), BF16)
    solved = apply_inverse(hi_ref[0], lo_ref[0], c_ref[0])
    width = solved.shape[1] // 2
    w_ref[0] = jnp.where(upper_ref[0] == 0, solved[:, :width], solved[:, width:])
    row = iota((HALF, BLK), 0)
    lane = iota((HALF, BLK), 1)
    from_low = lane - HALF < row
    eye = iota((BLK, BLK), 0) == iota((BLK, BLK), 1)
    extra_row = iota((EXTRA, BLK), 0)
    for r in range(groups):
        block = solved[:, r * BLK : (r + 1) * BLK]
        tile = mm_tn(block, block)
        folded = jnp.where(from_low, tile[HALF:], pltpu.roll(tile[:HALF], HALF, 1))
        diag = jnp.sum(jnp.where(eye, tile, 0.0), axis=0, keepdims=True)
        first = diag.astype(BF16).astype(F32)
        second = (diag - first).astype(BF16).astype(F32)
        third = diag - first - second
        extra = jnp.where(
            extra_row == 0,
            first,
            jnp.where(extra_row == 1, second, jnp.where(extra_row == 2, third, 0.0)),
        )
        d_ref[l * groups + r] = jnp.concatenate([folded, extra], axis=0).astype(BF16)


MESH = pl.DeviceIdType.MESH
SUB_SHAPE = (8, 4, 2)


def sub_peer(step):
    z_total, y_total, cores = SUB_SHAPE
    me = lax.axis_index("sub")
    z, y, core = me // (y_total * cores), (me // cores) % y_total, me % cores
    m = step % z_total
    dz = z_total // 2 + (1 - 2 * (m % 2)) * ((m + 1) // 2)
    rest = step // z_total
    return (
        ((z + dz) % z_total) * y_total + (y + rest // cores) % y_total
    ) * cores + (core + rest) % cores


def all_peers(total, act):
    skip = SUB_SHAPE[0] - 1

    def one(step, carry):
        act(sub_peer(step))
        return carry

    lax.fori_loop(0, skip, one, 0)
    lax.fori_loop(skip + 1, total, one, 0)


def greet(total, panels):
    barrier = pltpu.get_barrier_semaphore()
    panel = lax.axis_index("panel")

    def signal(peer):
        pl.semaphore_signal(barrier, inc=1, device_id={"sub": peer}, device_id_type=MESH)

    all_peers(total, signal)
    for away in range(1, panels):
        pl.semaphore_signal(
            barrier, inc=1, device_id={"panel": (panel + away) % panels}, device_id_type=MESH
        )
    return lambda: pl.semaphore_wait(barrier, total - 1 + panels - 1)


def to_panel(src, dst, send, recv, away):
    panels = lax.axis_size("panel")
    peer = (lax.axis_index("panel") + away) % panels
    return pltpu.make_async_remote_copy(
        src_ref=src,
        dst_ref=dst,
        send_sem=send,
        recv_sem=recv,
        device_id={"panel": peer},
        device_id_type=MESH,
    )


def await_bytes(ref, sem):
    pltpu.make_async_copy(ref, ref, sem).wait()


def scatter_slots(total, src_ref, tiles_ref, send_ref, recv_ref):
    me = lax.axis_index("sub")

    def one(s, carry):
        send_ref[s] = tiles_ref[src_ref[s]]
        return carry

    lax.fori_loop(0, total, one, 0, unroll=2)
    recv_ref[me] = tiles_ref[src_ref[me]]


def start_slots(total, send_ref, recv_ref, send, recv):
    me = lax.axis_index("sub")

    def go(peer):
        pltpu.make_async_remote_copy(
            src_ref=send_ref.at[peer],
            dst_ref=recv_ref.at[me],
            send_sem=send,
            recv_sem=recv,
            device_id={"sub": peer},
            device_id_type=MESH,
        ).start()

    all_peers(total, go)


def cross_products(first, count, pat_ref, hi_ref, lo_ref, c_ref, w_ref, x_ref, out_ref, send, recv):
    panels = lax.axis_size("panel")
    upper = lax.axis_index("panel") // (panels // 2)
    low = upper == 0
    width = c_ref.shape[2] // BLK

    def one(i, carry):
        solved = apply_inverse(hi_ref[i], lo_ref[i], c_ref[i])
        for r in range(width):
            own = w_ref[i, :, r * BLK : (r + 1) * BLK]
            other = solved[:, r * BLK : (r + 1) * BLK]
            tile = mm_tn(jnp.where(low, own, other), jnp.where(low, other, own))
            tile = tile * pat_ref[(first + i) * width + r].astype(F32)
            group = (first + i) * 2 * width + width * upper + r
            x_ref[group] = jnp.where(low, tile[:HALF], tile[HALF:]).astype(BF16)
            out_ref[i * width + r] = jnp.where(low, tile[HALF:], tile[:HALF]).astype(BF16)
            to_panel(
                out_ref.at[i * width + r], x_ref.at[group], send, recv, panels // 2
            ).start()
        return carry

    lax.fori_loop(0, count, one, 0)


def fetch(pairs, sem):
    copies = [pltpu.make_async_copy(src, dst, sem.at[k]) for k, (src, dst) in enumerate(pairs)]
    for copy in copies:
        copy.start()
    return copies


def first_kernel(
    count, src_ref, pat_ref, d_ref, icol_ref, hi_any, lo_any, c_any, w_any,
    got_ref, x_ref, cols_ref,
    dsend_ref, out_ref, hi_ref, lo_ref, c_ref, w_ref, local, slot_send, slot_recv, half_send, half_recv, col_send, col_recv,
):
    total = lax.axis_size("sub")
    panels = lax.axis_size("panel")
    panel = lax.axis_index("panel")
    rows = icol_ref.shape[0]
    ready = greet(total, panels)
    copies = fetch(
        [
            (hi_any.at[pl.ds(0, count)], hi_ref),
            (lo_any.at[pl.ds(0, count)], lo_ref),
            (c_any, c_ref),
            (w_any.at[pl.ds(0, count)], w_ref),
        ],
        local,
    )
    scatter_slots(total, src_ref, d_ref, dsend_ref, got_ref)
    ready()
    start_slots(total, dsend_ref, got_ref, slot_send, slot_recv)
    mine = cols_ref.at[pl.ds(pl.multiple_of(panel * rows, rows), rows)]
    column_copies = [
        to_panel(icol_ref, mine, col_send.at[away - 1], col_recv, away) for away in range(1, panels)
    ]
    for copy in column_copies:
        copy.start()
    cols_ref[pl.ds(pl.multiple_of(panel * rows, rows), rows), :] = icol_ref[...]
    for copy in copies:
        copy.wait()
    cross_products(0, count, pat_ref, hi_ref, lo_ref, c_ref, w_ref, x_ref, out_ref, half_send, half_recv)
    await_bytes(out_ref, half_send)
    await_bytes(out_ref, half_recv)
    for copy in column_copies:
        copy.wait_send()
    await_bytes(cols_ref.at[pl.ds(0, (panels - 1) * rows)], col_recv)
    await_bytes(dsend_ref.at[pl.ds(0, total - 1)], slot_send)
    await_bytes(got_ref.at[pl.ds(0, total - 1)], slot_recv)


def second_kernel(
    done, src_ref, pat_ref, dindex_ref, xindex_ref, dgot_ref, xin_ref, own_diag_ref, hi_any, lo_any, c_any, w_any,
    diag_ref, p_ref, inv_ref, pair_ref, col_ref,
    x_ref, xsend_ref, xgot_ref, out_ref, hi_ref, lo_ref, c_ref, w_ref, first_ref, a_ref, b_ref, t_ref,
    local, slot_send, slot_recv, half_send, half_recv, first_send, first_recv, pair_send, pair_recv, col_send, col_recv,
):
    total = lax.axis_size("sub")
    panels = lax.axis_size("panel")
    panel = lax.axis_index("panel")
    upper = panel // (panels // 2)
    count = c_ref.shape[0]
    ready = greet(total, panels)
    copies = fetch(
        [
            (hi_any.at[pl.ds(done, count)], hi_ref),
            (lo_any.at[pl.ds(done, count)], lo_ref),
            (c_any, c_ref),
            (w_any.at[pl.ds(done, count)], w_ref),
        ],
        local,
    )
    groups = xin_ref.shape[0]
    x_ref[:groups] = xin_ref[...]
    x_ref[x_ref.shape[0] - 1] = jnp.zeros(x_ref.shape[1:], BF16)
    ready()
    for copy in copies:
        copy.wait()
    cross_products(done, count, pat_ref, hi_ref, lo_ref, c_ref, w_ref, x_ref, out_ref, half_send, half_recv)
    await_bytes(out_ref, half_send)
    await_bytes(out_ref, half_recv)
    scatter_slots(total, src_ref, x_ref, xsend_ref, xgot_ref)
    start_slots(total, xsend_ref, xgot_ref, slot_send, slot_recv)

    sum_diagonal(dindex_ref, dgot_ref, own_diag_ref, diag_ref)

    @pl.when(panel == 0)
    def _():
        first_ref[...] = diag_ref[0]
        sends = [
            to_panel(first_ref, first_ref, first_send.at[away - 1], first_recv, away)
            for away in range(1, panels)
        ]
        for copy in sends:
            copy.start()
        for copy in sends:
            copy.wait_send()

    @pl.when(panel != 0)
    def _():
        await_bytes(first_ref, first_recv)

    factor_pivot(first_ref, p_ref, inv_ref, a_ref, b_ref, t_ref)
    await_bytes(xsend_ref.at[pl.ds(0, total - 1)], slot_send)
    await_bytes(xgot_ref.at[pl.ds(0, total - 1)], slot_recv)
    sum_cross(xindex_ref, xgot_ref, pair_ref, upper)
    pair = to_panel(pair_ref.at[upper], pair_ref.at[upper], pair_send, pair_recv, panels // 2)
    pair.start()

    @pl.when(panel % 2 == 0)
    def _():
        key = pair_ref.at[upper, pl.ds(0, 2)]
        sends = [
            to_panel(key, col_ref.at[upper], col_send.at[k], col_recv, away)
            for k, away in enumerate((1, panels - 1))
        ]
        for copy in sends:
            copy.start()
        for copy in sends:
            copy.wait_send()
        pair.wait()
        col_ref[...] = pair_ref[:, :2]

    @pl.when(panel % 2 == 1)
    def _():
        pair.wait()
        await_bytes(col_ref, col_recv)


def sum_diagonal(index_ref, recv_ref, own_diag_ref, out_ref):
    count, height, _ = recv_ref.shape
    places = out_ref.shape[0]

    def one(s, sums):
        value = recv_ref[s].astype(F32)
        at = index_ref[s]
        return tuple(
            total + jnp.where(at == r + 1, value, 0.0) for r, total in enumerate(sums)
        )

    start = tuple(jnp.zeros((height, BLK), F32) for _ in range(places))
    sums = lax.fori_loop(0, count, one, start, unroll=2)
    row = iota((HALF, BLK), 0)
    lane = iota((HALF, BLK), 1)
    eye = iota((BLK, BLK), 0) == iota((BLK, BLK), 1)
    for r in range(places):
        folded = sums[r][:HALF]
        low = jnp.where(lane - HALF < row, folded, 0.0)
        high = jnp.where(
            jnp.logical_and(lane > row, lane < HALF), pltpu.roll(folded, HALF, 1), 0.0
        )
        strict = jnp.concatenate([high, low], axis=0)
        diag = jnp.sum(sums[r][HALF:], axis=0, keepdims=True) + own_diag_ref[r : r + 1, :]
        out_ref[r] = strict + strict.T + jnp.where(eye, diag, 0.0)


def sum_cross(index_ref, recv_ref, out_ref, slot):
    count = recv_ref.shape[0]
    places = out_ref.shape[1]

    def one(s, sums):
        value = recv_ref[s].astype(F32)
        at = index_ref[s]
        return tuple(
            total + jnp.where(at == r + 1, value, 0.0) for r, total in enumerate(sums)
        )

    start = tuple(jnp.zeros((HALF, BLK), F32) for _ in range(places))
    sums = lax.fori_loop(0, count, one, start, unroll=2)
    for r in range(places):
        out_ref[slot, r] = sums[r]


def factor_pivot(tile_ref, p_ref, inv_ref, a_ref, b_ref, t_ref):
    step = 8
    a_ref[...] = tile_ref[...]
    b_ref[...] = jnp.where(iota((BLK, BLK), 0) == iota((BLK, BLK), 1), 1.0, 0.0)
    row = iota((BLK, BLK), 0)
    sub = iota((step, BLK), 0)
    lane = iota((step, BLK), 1)

    def group(g, carry):
        at = pl.ds(pl.multiple_of(g * step, step), step)
        a, b = a_ref[...], b_ref[...]
        rows, right = a_ref[at, :], b_ref[at, :]
        factor_rows, inverse_rows = [], []
        for s in range(step):
            pivot_row, right_row = rows[s : s + 1], right[s : s + 1]
            pivot = jnp.broadcast_to(pivot_row[:, s : s + 1], (1, BLK))
            root = 1.0 / jnp.sqrt(pivot)
            inverse = 1.0 / pivot
            factor_rows.append(pivot_row * root)
            inverse_rows.append(right_row * root)
            scaled, right_scaled = pivot_row * inverse, right_row * inverse
            near = jnp.where(sub > s, rows[:, s : s + 1], 0.0)
            far = jnp.where(row > g * step + s, a[:, s : s + 1], 0.0)
            rows, right = rows - near * scaled, right - near * right_scaled
            a, b = a - far * scaled, b - far * right_scaled
        a_ref[...] = pltpu.roll(a, BLK - step, 1)
        b_ref[...] = b
        block = jnp.concatenate(factor_rows, axis=0)
        block = jnp.where(jnp.logical_and(lane >= sub, lane < BLK - g * step), block, 0.0)
        t_ref[at, :] = pltpu.roll(block, g * step, 1)
        inv_ref[at, :] = jnp.concatenate(inverse_rows, axis=0)
        return carry

    lax.fori_loop(0, BLK // step, group, 0)
    p_ref[...] = t_ref[...].T


def final_kernel(panel_ref, diag_ref, pair_ref, col_ref, icol_ref, p_ref, inv_ref, asm_ref, fac_ref, l_ref):
    panel = panel_ref[0]
    lower = panel < 2
    other = (panel + 2) % 4
    asm_ref[...] = jnp.zeros_like(asm_ref)
    for r in range(2):
        at = pl.multiple_of((panel * 2 + r) * BLK, BLK)
        asm_ref[r * BLK : (r + 1) * BLK, pl.ds(at, BLK)] = diag_ref[r]
    for a in range(2):
        for b in range(2):
            tile = jnp.concatenate([pair_ref[0, a * 2 + b], pair_ref[1, a * 2 + b]], axis=0)
            tile = jnp.where(lower, tile, tile.T)
            row = pl.multiple_of(jnp.where(lower, a, b) * BLK, BLK)
            at = pl.multiple_of((other * 2 + jnp.where(lower, b, a)) * BLK, BLK)
            asm_ref[pl.ds(row, BLK), pl.ds(at, BLK)] = tile
    own = pl.multiple_of(panel * 2 * BLK, BLK)
    off = jnp.logical_or(panel > 0, iota((2 * BLK, BLK), 0) >= BLK)
    asm_ref[:, :BLK] = asm_ref[:, :BLK] + jnp.where(off, icol_ref[pl.ds(own, 2 * BLK), :], 0.0)
    inv_hi, inv_lo = split(inv_ref[...])
    l_ref[:BLK, :] = p_ref[...]
    for r in range(1, OWN):
        key = icol_ref[r * BLK : (r + 1) * BLK, :]
        if r in (4, 5):
            key = key + jnp.concatenate([col_ref[0, r - 4], col_ref[1, r - 4]], axis=0).T
        kh, kl = split(key)
        l_ref[r * BLK : (r + 1) * BLK, :] = mm_nt(kh, inv_hi) + (
            mm_nt(kh, inv_lo) + mm_nt(kl, inv_hi)
        )
    mine = l_ref[pl.ds(own, 2 * BLK), :]
    mh, ml = split(mine)
    fac_ref[:, :BLK] = mine
    for c in range(1, OWN):
        lh, ll = split(l_ref[c * BLK : (c + 1) * BLK, :])
        update = mm_nt(mh, lh) + (mm_nt(mh, ll) + mm_nt(ml, lh))
        fac_ref[:, c * BLK : (c + 1) * BLK] = asm_ref[:, c * BLK : (c + 1) * BLK] - jnp.where(
            off, update, 0.0
        )


def cost(flops, nbytes):
    return pl.CostEstimate(flops=flops, bytes_accessed=nbytes, transcendentals=0)


def whole(count):
    return [pl.BlockSpec(memory_space=VMEM)] * count


SMEM = pl.BlockSpec(memory_space=pltpu.SMEM)


def partner(value, panels):
    pairs = [(source, (source + panels // 2) % panels) for source in range(panels)]
    return lax.ppermute(value, "panel", pairs)


def per_device(
    interior_factor, coupling, interface_diag, interface_column, block_map, pair_pattern
):
    subs, order, width = coupling.shape
    owners_total = lax.axis_size("sub")
    panels = lax.axis_size("panel")
    sub = lax.axis_index("sub")
    panel = lax.axis_index("panel")
    upper = (panel >= panels // 2).astype(jnp.int32)
    upper_s = upper.reshape(1)
    panel_s = panel.astype(jnp.int32).reshape(1)
    groups = width // BLK
    half_width = width // 2

    outgoing = lax.dynamic_slice_in_dim(coupling, (1 - upper) * half_width, half_width, 2)
    incoming = [partner(outgoing[:EARLY], panels), partner(outgoing[EARLY:], panels)]

    maps = block_map.reshape(owners_total, subs, panels, groups)
    owner = maps[:, :, 0, :] // OWN
    match = (owner == sub).astype(jnp.int32)
    place = maps % 2
    base = panel % 2
    own_place = lax.dynamic_index_in_dim(place, panel, 2, keepdims=False)
    low_place = lax.dynamic_index_in_dim(place, base, 2, keepdims=False)
    high_place = lax.dynamic_index_in_dim(place, base + 2, 2, keepdims=False)
    diag_index = jnp.sum(match * (1 + own_place), axis=(1, 2))
    cross_index = jnp.sum(match * (1 + 2 * low_place + high_place), axis=(1, 2))
    slots = lax.dynamic_index_in_dim(owner, sub, 0, keepdims=False).reshape(-1)
    tiles = subs * groups
    filled = (slots[None, :] == jnp.arange(owners_total, dtype=jnp.int32)[:, None]).astype(jnp.int32)
    source = tiles + jnp.sum(
        filled * (jnp.arange(tiles, dtype=jnp.int32) - tiles)[None, :], axis=1
    )
    pattern = lax.dynamic_slice_in_dim(pair_pattern, base * groups + upper * 2, 2, 1).reshape(-1)

    hi, lo, w_half, diag_tiles = pl.pallas_call(
        solve_kernel,
        grid=(subs,),
        in_specs=[
            SMEM,
            pl.BlockSpec((subs, order, order), lambda l: (0, 0, 0)),
            pl.BlockSpec((1, order, width), lambda l: (l, 0, 0)),
        ],
        out_specs=[
            pl.BlockSpec((1, order, order), lambda l: (l, 0, 0)),
            pl.BlockSpec((1, order, order), lambda l: (l, 0, 0)),
            pl.BlockSpec((1, order, half_width), lambda l: (l, 0, 0)),
            pl.BlockSpec((tiles + 1, HALF + EXTRA, BLK), lambda l: (0, 0, 0)),
        ],
        out_shape=[
            jax.ShapeDtypeStruct((subs, order, order), BF16),
            jax.ShapeDtypeStruct((subs, order, order), BF16),
            jax.ShapeDtypeStruct((subs, order, half_width), BF16),
            jax.ShapeDtypeStruct((tiles + 1, HALF + EXTRA, BLK), BF16),
        ],
        scratch_shapes=[
            VMEM((subs * order, BLK), F32),
            VMEM((BASE, BASE, BLK), F32),
            VMEM((BASE, BASE, BLK), F32),
        ],
        compiler_params=pltpu.CompilerParams(vmem_limit_bytes=48 * 2**20),
        cost_estimate=cost(2 * 10**10, 2**25),
        name="solve",
    )(upper_s, interior_factor, coupling)

    anywhere = pl.BlockSpec(memory_space=pl.ANY)
    dma = pltpu.SemaphoreType.DMA

    def staged(count):
        return [
            VMEM((count, order, order), BF16),
            VMEM((count, order, order), BF16),
            VMEM((count, order, half_width), BF16),
            VMEM((count, order, half_width), BF16),
        ]

    diag_got, cross_early, columns = pl.pallas_call(
        functools.partial(first_kernel, EARLY),
        in_specs=[SMEM] * 2 + whole(2) + [anywhere] * 4,
        out_specs=whole(3),
        out_shape=[
            jax.ShapeDtypeStruct((owners_total, HALF + EXTRA, BLK), BF16),
            jax.ShapeDtypeStruct((EARLY * groups, HALF, BLK), BF16),
            jax.ShapeDtypeStruct((OWN * BLK, BLK), F32),
        ],
        scratch_shapes=[
            VMEM((owners_total, HALF + EXTRA, BLK), BF16),
            VMEM((EARLY * 2, HALF, BLK), BF16),
            *staged(EARLY),
            dma((4,)),
            dma,
            dma,
            dma,
            dma,
            dma((panels - 1,)),
            dma,
        ],
        compiler_params=pltpu.CompilerParams(
            collective_id=1, has_side_effects=True, vmem_limit_bytes=48 * 2**20
        ),
        cost_estimate=cost(10**10, 2**24),
        name="first",
    )(source, pattern, diag_tiles, interface_column, hi, lo, incoming[0], w_half)

    rows = OWN // panels
    late = subs - EARLY
    diag, pivot, pivot_inverse, pair, col = pl.pallas_call(
        functools.partial(second_kernel, EARLY),
        in_specs=[SMEM] * 4 + whole(3) + [anywhere] * 4,
        out_specs=whole(5),
        out_shape=[
            jax.ShapeDtypeStruct((rows, BLK, BLK), F32),
            jax.ShapeDtypeStruct((BLK, BLK), F32),
            jax.ShapeDtypeStruct((BLK, BLK), F32),
            jax.ShapeDtypeStruct((2, rows * rows, HALF, BLK), F32),
            jax.ShapeDtypeStruct((2, 2, HALF, BLK), F32),
        ],
        scratch_shapes=[
            VMEM((tiles + 1, HALF, BLK), BF16),
            VMEM((owners_total, HALF, BLK), BF16),
            VMEM((owners_total, HALF, BLK), BF16),
            VMEM((late * 2, HALF, BLK), BF16),
            *staged(late),
            VMEM((BLK, BLK), F32),
            VMEM((BLK, BLK), F32),
            VMEM((BLK, BLK), F32),
            VMEM((BLK, BLK), F32),
            dma((4,)),
            dma,
            dma,
            dma,
            dma,
            dma((panels - 1,)),
            dma,
            dma,
            dma,
            dma((2,)),
            dma,
        ],
        compiler_params=pltpu.CompilerParams(
            collective_id=2, has_side_effects=True, vmem_limit_bytes=48 * 2**20
        ),
        cost_estimate=cost(10**10, 2**24),
        name="second",
    )(
        source, pattern, diag_index, cross_index, diag_got, cross_early,
        interface_diag.reshape(rows, BLK), hi, lo, incoming[1], w_half,
    )
    return pl.pallas_call(
        final_kernel,
        in_specs=[SMEM] + whole(6),
        out_specs=whole(2),
        out_shape=[jax.ShapeDtypeStruct((rows * BLK, OWN * BLK), F32)] * 2,
        scratch_shapes=[VMEM((OWN * BLK, BLK), F32)],
        cost_estimate=cost(10**9, 2**22),
        name="final",
    )(panel_s, diag, pair, col, columns, pivot, pivot_inverse)


def solution(mesh):
    return jax.shard_map(
        per_device,
        mesh=mesh,
        in_specs=(
            P("sub", None, None),
            P("sub", None, "panel"),
            P(("sub", "panel")),
            P(("sub", "panel"), None),
            P(),
            P("sub", None),
        ),
        out_specs=(P(("sub", "panel"), None), P(("sub", "panel"), None)),
        check_vma=False,
    )
```

time: 151 us -> 133 us (0.88)
  Pallas kernels: 62.9 us -> 118 us
  blocking collectives: 39.9 us -> 0 us
  starting transfers between devices: 24.1 us -> 3.53 us
  waiting for transfers between devices: 13.8 us -> 0.01 us
    pallas_call x6 -> x3, Pallas kernels: 59.1 us -> 114 us  [the longest x1 46.1 us: per_device(): pl.pallas_call(functools.partial(second_kernel, EARLY), in_specs=[SMEM] *...]
    all_gather x3 -> x0, blocking collectives: 39.9 us -> none  [the longest x1 14 us: per_device(): all_halves = lax.all_gather(halves, 'panel', axis=0)]
    all_to_all x2 -> x0, starting transfers between devices: 17.9 us -> none  [the longest x1 12.3 us: per_device(): lax.all_to_all(diag_send, 'sub', split_axis=0, concat_axis=0, tiled=True)]
    all_to_all x2 -> x0, waiting for transfers between devices: 7.66 us -> none  [the longest x1 7.66 us: per_device(): lax.all_to_all(diag_send, 'sub', split_axis=0, concat_axis=0, tiled=True)]
    ppermute x2, waiting for transfers between devices: 6.11 us -> 0.01 us  [partner(): return lax.ppermute(value, 'panel', pairs)]
    slice x1 -> x2, local copies, waits for them, and re-layouts: 0.84 us -> 4.6 us  [the longest x1 2.54 us: per_device(): outgoing[:EARLY]]
    ppermute x2, starting transfers between devices: 6.14 us -> 3.53 us  [partner(): return lax.ppermute(value, 'panel', pairs)]
    dynamic_slice x6 -> x2, local copies, waits for them, and re-layouts: 1.99 us -> 0.1 us  [per_device(): slots = lax.dynamic_index_in_dim(owner, sub, 0, keepdims=False).reshape(-1)]
  transfers between devices with their start and end apart: 4 -> 2, of which waited for: 3 -> 0; matrix products, arithmetic and copies ran while one was open for 3% -> 2% of each run, Pallas kernels for 38% -> 52%
where the time goes in v2:
time: 133 us; the launch traced here: 131 us
  Pallas kernels  118 us (89%)
  local copies, waits for them, and re-layouts  8.48 us (6%)
  starting transfers between devices  3.53 us (3%)
    pallas_call x1, Pallas kernels, per_device(): pl.pallas_call(functools.partial(second_kernel, EARLY), in_specs=[SMEM] *...  46.1 us
    pallas_call x1, Pallas kernels, per_device(): pl.pallas_call(functools.partial(first_kernel, EARLY), in_specs=[SMEM] *...  39.2 us
    pallas_call x1, Pallas kernels, per_device(): pl.pallas_call(solve_kernel, grid=(subs,), in_specs=[SMEM, pl.BlockSpec((...  29.1 us
    pallas_call x1, Pallas kernels, per_device(): pl.pallas_call(final_kernel, in_specs=[SMEM] + whole(6), out_specs=whole(...  3.7 us
    ppermute x2, starting transfers between devices, partner(): return lax.ppermute(value, 'panel', pairs)  3.53 us
    unnamed x20, local copies, waits for them, and re-layouts  3.25 us
  transfers between devices with their start and end apart: 2, of which 0 were waited for; matrix products, arithmetic and copies ran while one was open for 2% of the time, Pallas kernels for 52%

profile of v2, /device:TPU:8, one launch (start us, length us, event | category | flops | bytes accessed | tf_op | source)
XLA Modules:
  0.0 131.5 jit_solution(2859587378112400201)
XLA Ops:
  0.6 0.0 copy-start
  0.6 0.0 copy-start.9
  0.7 2.5 %constant_dynamic-slice_fusion = bf16[5,512,256]{2,1,0:T(8,128)(2,1)} fusion(bf16[8,512,512]{2,1,0:T(8,128)(2,1)} %c_ref.1, s32[]{:T(128)S(6)} %select_n.46), kind=kLoop, calls=%fused_computation.19 | loop fusion | bytes 2621444 | tf_op jit(solution)/shard_map/slice | solution.py:572
  3.2 3.0 %collective-permute-start = (bf16[5,512,256]{2,1,0:T(8,128)(2,1)}, bf16[5,512,256]{2,1,0:T(8,128)(2,1)S(1)}, u32[]{:S(2)}, u32[]{:S(2)}) collective-permute-start(bf16[5,512,256]{2,1,0:T(8,128)(2,1)} %constant_dynamic-slice_fusion), channel_id=1, source_target_pairs={{0,2},{1,3},{2,0},{3,1},{4,6},{5,7},{6,4},{7,5},{8,10},{9,11},{10,... | collective-permute-start | bytes 3932168 | tf_op jit(solution)/shard_map/ppermute | solution.py:554
  6.2 2.1 %constant_dynamic-slice_fusion.1 = bf16[3,512,256]{2,1,0:T(8,128)(2,1)} fusion(bf16[8,512,512]{2,1,0:T(8,128)(2,1)} %c_ref.1, s32[]{:T(128)S(6)} %add.83, s32[]{:T(128)S(6)} %select_n.46), kind=kLoop, calls=%fused_computation.20 | loop fusion | bytes 1572872 | tf_op jit(solution)/shard_map/slice | solution.py:572
  8.3 0.5 collective-permute-start.1
  8.8 0.0 copy-done.9
  8.8 0.3 reshape.33
  9.1 0.1 broadcast_compare_fusion
  9.2 0.2 add_select_fusion
  9.5 0.1 copy.13
  9.5 0.1 eq.25
  9.6 0.1 select_reduce_fusion
  9.7 0.0 copy-done
  9.7 0.1 constant_dynamic-slice_fusion.2
  9.8 0.1 reshape.34.pat_ref
  9.9 0.2 fusion.2
  10.0 0.0 copy-start.1
  10.1 29.1 %solve.1 = (bf16[8,512,512]{2,1,0:T(8,128)(2,1)}, bf16[8,512,512]{2,1,0:T(8,128)(2,1)}, bf16[8,512,256]{2,1,0:T(8,128)(2,1)S(1)}, bf16[33,72,128]{2,1,0:T(8,128)(2,1)S(1)}) custom-call(s32[1]{0:T(128)} %bitcast.4.upper_ref, f32[8,512,512]{2,1,0:T(8,128)} %f_ref.1, bf16[8,512,512]{2,1,0:T(8,128)(2,1)} %c_ref.1), custom_call_target="tpu_custom_call" | custom-call | flops 20000000000 | bytes 33554432 | tf_op jit(solution)/shard_map/solve/pallas_call | solution.py:592
  39.2 0.0 collective-permute-done.c_any
  39.2 0.0 copy-done.1
  39.2 0.0 copy-start.2
  39.2 39.2 %first.1 = (bf16[64,72,128]{2,1,0:T(8,128)(2,1)S(1)}, bf16[20,64,128]{2,1,0:T(8,128)(2,1)S(1)}, f32[1024,128]{1,0:T(8,128)S(1)}) custom-call(s32[64]{0:T(128)S(1)} %broadcast_add_fusion.src_ref, s32[16]{0:T(128)S(1)} %reshape.34.pat_ref, bf16[33,72,128]{2,1,0:T(8,128)(2,1)S(1)} %get-tuple-element.14.d_ref, f32[256,128]{1,0:T(8,128)S(1)} %copy-done.1, ...), custom_call_target="tpu_custom_call" | custom-call | flops 10000000000 | bytes 16777216 | tf_op jit(solution)/shard_map/first/pallas_call | solution.py:633
  78.4 0.0 copy-start.3
  78.4 0.0 collective-permute-done.1.c_any
  78.4 0.0 copy-done.2
  78.4 46.1 %second.1 = (f32[2,128,128]{2,1,0:T(8,128)S(1)}, f32[128,128]{1,0:T(8,128)S(1)}, f32[128,128]{1,0:T(8,128)S(1)}, f32[2,4,64,128]{3,2,1,0:T(8,128)S(1)}, f32[2,2,64,128]{3,2,1,0:T(8,128)S(1)}) custom-call(s32[64]{0:T(128)S(1)} %broadcast_add_fusion.src_ref, s32[16]{0:T(128)S(1)} %reshape.34.pat_ref, s32[64]{0:T(128)S(1)} %get-tuple-element.27.dindex_ref, ...), custom_call_target="tpu_custom_call" | custom-call | flops 10000000000 | bytes 16777216 | tf_op jit(solution)/shard_map/second/pallas_call | solution.py:663
  124.6 0.0 copy-done.3
  124.6 0.0 copy-start.4
  124.6 0.7 copy-done.4
  125.3 0.0 copy-start.5
  125.3 0.6 copy-done.5
  125.9 0.0 copy-start.6
  125.9 0.7 copy-done.6
  126.5 0.0 copy-start.7
  126.6 0.6 copy-done.7
  127.2 0.0 copy-start.8
  127.2 0.6 copy-done.8
  127.8 3.7 %final.1 = (f32[256,1024]{1,0:T(8,128)}, f32[256,1024]{1,0:T(8,128)}) custom-call(s32[1]{0:T(128)} %bitcast.panel_ref, f32[2,128,128]{2,1,0:T(8,128)} %copy-done.5, f32[2,4,64,128]{3,2,1,0:T(8,128)} %copy-done.4, f32[2,2,64,128]{3,2,1,0:T(8,128)} %copy-done.6, f32[1024,128]{1,0:T(8,128)} %copy-done.3, f32[128,128]{1,0:T(8,128)} %copy-done.7, ...), custom_call_target="tpu_custom_call" | custom-call | flops 1000000000 | bytes 4194304 | tf_op jit(solution)/shard_map/final/pallas_call | solution.py:705
  (3 shorter events, 0.0 us)
Async XLA Ops:
  0.6 9.1 %copy-start = (s32[8,8]{1,0:T(8,128)S(1)}, s32[8,8]{1,0:T(8,128)}, u32[]{:S(2)}) copy-start(s32[8,8]{1,0:T(8,128)} %param.11) | copy-start | bytes 772
  0.6 8.2 %copy-start.9 = (s32[512,16]{0,1:T(8,128)S(1)}, s32[512,16]{0,1:T(8,128)}, u32[]{:S(2)}) copy-start(s32[512,16]{0,1:T(8,128)} %param.10) | copy-start | bytes 98308
  3.2 36.0 %collective-permute-start = (bf16[5,512,256]{2,1,0:T(8,128)(2,1)}, bf16[5,512,256]{2,1,0:T(8,128)(2,1)S(1)}, u32[]{:S(2)}, u32[]{:S(2)}) collective-permute-start(bf16[5,512,256]{2,1,0:T(8,128)(2,1)} %constant_dynamic-slice_fusion), channel_id=1, source_target_pairs={{0,2},{1,3},{2,0},{3,1},{4,6},{5,7},{6,4},{7,5},{8,10},{9,11},{10,... | collective-permute-start | bytes 3932168 | tf_op jit(solution)/shard_map/ppermute | solution.py:554
  8.3 70.1 %collective-permute-start.1 = (bf16[3,512,256]{2,1,0:T(8,128)(2,1)}, bf16[3,512,256]{2,1,0:T(8,128)(2,1)S(1)}, u32[]{:S(2)}, u32[]{:S(2)}) collective-permute-start(bf16[3,512,256]{2,1,0:T(8,128)(2,1)} %constant_dynamic-slice_fusion.1), channel_id=1, source_target_pairs={{0,2},{1,3},{2,0},{3,1},{4,6},{5,7},{6,4},{7,5},{8,10},{9,11},{10,... | collective-permute-start | bytes 2359304 | tf_op jit(solution)/shard_map/ppermute | solution.py:554
  10.0 29.1 %copy-start.1 = (f32[256,128]{1,0:T(8,128)S(1)}, f32[256,128]{1,0:T(8,128)}, u32[]{:S(2)}) copy-start(f32[256,128]{1,0:T(8,128)} %icol_ref.1) | copy-start | bytes 393220
  39.2 39.2 %copy-start.2 = (f32[256]{0:T(256)S(1)}, f32[256]{0:T(256)}, u32[]{:S(2)}) copy-start(f32[256]{0:T(256)} %param.8) | copy-start | bytes 3076
  78.4 46.2 %copy-start.3 = (f32[1024,128]{1,0:T(8,128)}, f32[1024,128]{1,0:T(8,128)S(1)}, u32[]{:S(2)}) copy-start(f32[1024,128]{1,0:T(8,128)S(1)} %get-tuple-element.23.icol_ref) | copy-start | bytes 1572868
  124.6 0.7 copy-start.4
  125.3 0.6 copy-start.5
  125.9 0.7 copy-start.6
  126.5 0.6 copy-start.7
  127.2 0.6 copy-start.8

commit v3 on v2

--- a/solution.py
+++ b/solution.py
@@ -268,111 +268,87 @@
     all_peers(total, go)
 
 
-def cross_products(first, count, pat_ref, hi_ref, lo_ref, c_ref, w_ref, x_ref, out_ref, send, recv):
+def cross_product(l, i, pat_ref, hi_ref, lo_ref, c_ref, w_ref, x_ref, out_ref, send, recv):
     panels = lax.axis_size("panel")
     upper = lax.axis_index("panel") // (panels // 2)
     low = upper == 0
     width = c_ref.shape[2] // BLK
-
-    def one(i, carry):
-        solved = apply_inverse(hi_ref[i], lo_ref[i], c_ref[i])
-        for r in range(width):
-            own = w_ref[i, :, r * BLK : (r + 1) * BLK]
-            other = solved[:, r * BLK : (r + 1) * BLK]
-            tile = mm_tn(jnp.where(low, own, other), jnp.where(low, other, own))
-            tile = tile * pat_ref[(first + i) * width + r].astype(F32)
-            group = (first + i) * 2 * width + width * upper + r
-            x_ref[group] = jnp.where(low, tile[:HALF], tile[HALF:]).astype(BF16)
-            out_ref[i * width + r] = jnp.where(low, tile[HALF:], tile[:HALF]).astype(BF16)
-            to_panel(
-                out_ref.at[i * width + r], x_ref.at[group], send, recv, panels // 2
-            ).start()
-        return carry
-
-    lax.fori_loop(0, count, one, 0)
-
-
-def fetch(pairs, sem):
-    copies = [pltpu.make_async_copy(src, dst, sem.at[k]) for k, (src, dst) in enumerate(pairs)]
-    for copy in copies:
-        copy.start()
-    return copies
-
-
-def first_kernel(
-    count, src_ref, pat_ref, d_ref, icol_ref, hi_any, lo_any, c_any, w_any,
-    got_ref, x_ref, cols_ref,
-    dsend_ref, out_ref, hi_ref, lo_ref, c_ref, w_ref, local, slot_send, slot_recv, half_send, half_recv, col_send, col_recv,
-):
-    total = lax.axis_size("sub")
-    panels = lax.axis_size("panel")
-    panel = lax.axis_index("panel")
-    rows = icol_ref.shape[0]
-    ready = greet(total, panels)
-    copies = fetch(
-        [
-            (hi_any.at[pl.ds(0, count)], hi_ref),
-            (lo_any.at[pl.ds(0, count)], lo_ref),
-            (c_any, c_ref),
-            (w_any.at[pl.ds(0, count)], w_ref),
-        ],
-        local,
-    )
-    scatter_slots(total, src_ref, d_ref, dsend_ref, got_ref)
-    ready()
-    start_slots(total, dsend_ref, got_ref, slot_send, slot_recv)
-    mine = cols_ref.at[pl.ds(pl.multiple_of(panel * rows, rows), rows)]
-    column_copies = [
-        to_panel(icol_ref, mine, col_send.at[away - 1], col_recv, away) for away in range(1, panels)
-    ]
-    for copy in column_copies:
-        copy.start()
-    cols_ref[pl.ds(pl.multiple_of(panel * rows, rows), rows), :] = icol_ref[...]
-    for copy in copies:
-        copy.wait()
-    cross_products(0, count, pat_ref, hi_ref, lo_ref, c_ref, w_ref, x_ref, out_ref, half_send, half_recv)
-    await_bytes(out_ref, half_send)
-    await_bytes(out_ref, half_recv)
-    for copy in column_copies:
-        copy.wait_send()
-    await_bytes(cols_ref.at[pl.ds(0, (panels - 1) * rows)], col_recv)
-    await_bytes(dsend_ref.at[pl.ds(0, total - 1)], slot_send)
-    await_bytes(got_ref.at[pl.ds(0, total - 1)], slot_recv)
-
-
-def second_kernel(
-    done, src_ref, pat_ref, dindex_ref, xindex_ref, dgot_ref, xin_ref, own_diag_ref, hi_any, lo_any, c_any, w_any,
-    diag_ref, p_ref, inv_ref, pair_ref, col_ref,
-    x_ref, xsend_ref, xgot_ref, out_ref, hi_ref, lo_ref, c_ref, w_ref, first_ref, a_ref, b_ref, t_ref,
-    local, slot_send, slot_recv, half_send, half_recv, first_send, first_recv, pair_send, pair_recv, col_send, col_recv,
+    solved = apply_inverse(hi_ref[l], lo_ref[l], c_ref[i])
+    for r in range(width):
+        own = w_ref[l, :, r * BLK : (r + 1) * BLK]
+        other = solved[:, r * BLK : (r + 1) * BLK]
+        tile = mm_tn(jnp.where(low, own, other), jnp.where(low, other, own))
+        tile = tile * pat_ref[l * width + r].astype(F32)
+        group = l * 2 * width + width * upper + r
+        x_ref[group] = jnp.where(low, tile[:HALF], tile[HALF:]).astype(BF16)
+        out_ref[l * width + r] = jnp.where(low, tile[HALF:], tile[:HALF]).astype(BF16)
+        to_panel(
+            out_ref.at[l * width + r], x_ref.at[group], send, recv, panels // 2
+        ).start()
+
+
+def exchange_kernel(
+    src_ref, pat_ref, dindex_ref, xindex_ref, d_ref, icol_ref, own_diag_ref,
+    hi_ref, lo_ref, early_ref, w_ref, c_any,
+    diag_ref, p_ref, inv_ref, pair_ref, col_ref, cols_ref,
+    dsend_ref, dgot_ref, x_ref, out_ref, xsend_ref, xgot_ref,
+    late_ref, first_ref, a_ref, b_ref, t_ref,
+    late_send, late_recv, dslot_send, dslot_recv, slot_send, slot_recv, half_send, half_recv,
+    cols_send, cols_recv, first_send, first_recv, pair_send, pair_recv, col_send, col_recv,
 ):
     total = lax.axis_size("sub")
     panels = lax.axis_size("panel")
     panel = lax.axis_index("panel")
     upper = panel // (panels // 2)
-    count = c_ref.shape[0]
+    early, late = early_ref.shape[0], late_ref.shape[0]
+    half_width = late_ref.shape[2]
+    rows = icol_ref.shape[0]
     ready = greet(total, panels)
-    copies = fetch(
-        [
-            (hi_any.at[pl.ds(done, count)], hi_ref),
-            (lo_any.at[pl.ds(done, count)], lo_ref),
-            (c_any, c_ref),
-            (w_any.at[pl.ds(done, count)], w_ref),
-        ],
-        local,
-    )
-    groups = xin_ref.shape[0]
-    x_ref[:groups] = xin_ref[...]
+    scatter_slots(total, src_ref, d_ref, dsend_ref, dgot_ref)
+    ready()
+    at = pl.multiple_of((1 - upper) * half_width, half_width)
+    late_copies = [
+        to_panel(
+            c_any.at[early + i, :, pl.ds(at, half_width)],
+            late_ref.at[i],
+            late_send.at[i],
+            late_recv.at[i],
+            panels // 2,
+        )
+        for i in range(late)
+    ]
+    for copy in late_copies:
+        copy.start()
+    start_slots(total, dsend_ref, dgot_ref, dslot_send, dslot_recv)
+    mine = pl.ds(pl.multiple_of(panel * rows, rows), rows)
+    column_copies = [
+        to_panel(icol_ref, cols_ref.at[mine], cols_send.at[away - 1], cols_recv, away)
+        for away in range(1, panels)
+    ]
+    for copy in column_copies:
+        copy.start()
+    cols_ref[mine, :] = icol_ref[...]
+
+    def cross_early(i, carry):
+        cross_product(
+            i, i, pat_ref, hi_ref, lo_ref, early_ref, w_ref, x_ref, out_ref, half_send, half_recv
+        )
+        return carry
+
+    lax.fori_loop(0, early, cross_early, 0)
+    for i in range(late):
+        late_copies[i].wait()
+        cross_product(
+            early + i, i, pat_ref, hi_ref, lo_ref, late_ref, w_ref, x_ref, out_ref, half_send, half_recv
+        )
     x_ref[x_ref.shape[0] - 1] = jnp.zeros(x_ref.shape[1:], BF16)
-    ready()
-    for copy in copies:
-        copy.wait()
-    cross_products(done, count, pat_ref, hi_ref, lo_ref, c_ref, w_ref, x_ref, out_ref, half_send, half_recv)
     await_bytes(out_ref, half_send)
     await_bytes(out_ref, half_recv)
     scatter_slots(total, src_ref, x_ref, xsend_ref, xgot_ref)
     start_slots(total, xsend_ref, xgot_ref, slot_send, slot_recv)
 
+    await_bytes(dsend_ref.at[pl.ds(0, total - 1)], dslot_send)
+    await_bytes(dgot_ref.at[pl.ds(0, total - 1)], dslot_recv)
     sum_diagonal(dindex_ref, dgot_ref, own_diag_ref, diag_ref)
 
     @pl.when(panel == 0)
@@ -392,6 +368,9 @@
         await_bytes(first_ref, first_recv)
 
     factor_pivot(first_ref, p_ref, inv_ref, a_ref, b_ref, t_ref)
+    for copy in column_copies:
+        copy.wait_send()
+    await_bytes(cols_ref.at[pl.ds(0, (panels - 1) * rows)], cols_recv)
     await_bytes(xsend_ref.at[pl.ds(0, total - 1)], slot_send)
     await_bytes(xgot_ref.at[pl.ds(0, total - 1)], slot_recv)
     sum_cross(xindex_ref, xgot_ref, pair_ref, upper)
@@ -568,8 +547,10 @@
     groups = width // BLK
     half_width = width // 2
 
-    outgoing = lax.dynamic_slice_in_dim(coupling, (1 - upper) * half_width, half_width, 2)
-    incoming = [partner(outgoing[:EARLY], panels), partner(outgoing[EARLY:], panels)]
+    outgoing = lax.dynamic_slice(
+        coupling, (0, 0, (1 - upper) * half_width), (EARLY, order, half_width)
+    )
+    incoming = partner(outgoing, panels)
 
     maps = block_map.reshape(owners_total, subs, panels, groups)
     owner = maps[:, :, 0, :] // OWN
@@ -614,7 +595,7 @@
             VMEM((BASE, BASE, BLK), F32),
             VMEM((BASE, BASE, BLK), F32),
         ],
-        compiler_params=pltpu.CompilerParams(vmem_limit_bytes=48 * 2**20),
+        compiler_params=pltpu.CompilerParams(vmem_limit_bytes=40 * 2**20),
         cost_estimate=cost(2 * 10**10, 2**25),
         name="solve",
     )(upper_s, interior_factor, coupling)
@@ -622,85 +603,49 @@
     anywhere = pl.BlockSpec(memory_space=pl.ANY)
     dma = pltpu.SemaphoreType.DMA
 
-    def staged(count):
-        return [
-            VMEM((count, order, order), BF16),
-            VMEM((count, order, order), BF16),
-            VMEM((count, order, half_width), BF16),
-            VMEM((count, order, half_width), BF16),
-        ]
-
-    diag_got, cross_early, columns = pl.pallas_call(
-        functools.partial(first_kernel, EARLY),
-        in_specs=[SMEM] * 2 + whole(2) + [anywhere] * 4,
-        out_specs=whole(3),
-        out_shape=[
-            jax.ShapeDtypeStruct((owners_total, HALF + EXTRA, BLK), BF16),
-            jax.ShapeDtypeStruct((EARLY * groups, HALF, BLK), BF16),
-            jax.ShapeDtypeStruct((OWN * BLK, BLK), F32),
-        ],
-        scratch_shapes=[
-            VMEM((owners_total, HALF + EXTRA, BLK), BF16),
-            VMEM((EARLY * 2, HALF, BLK), BF16),
-            *staged(EARLY),
-            dma((4,)),
-            dma,
-            dma,
-            dma,
-            dma,
-            dma((panels - 1,)),
-            dma,
-        ],
-        compiler_params=pltpu.CompilerParams(
-            collective_id=1, has_side_effects=True, vmem_limit_bytes=48 * 2**20
-        ),
-        cost_estimate=cost(10**10, 2**24),
-        name="first",
-    )(source, pattern, diag_tiles, interface_column, hi, lo, incoming[0], w_half)
-
     rows = OWN // panels
     late = subs - EARLY
-    diag, pivot, pivot_inverse, pair, col = pl.pallas_call(
-        functools.partial(second_kernel, EARLY),
-        in_specs=[SMEM] * 4 + whole(3) + [anywhere] * 4,
-        out_specs=whole(5),
+    slot_shape = (owners_total, HALF, BLK)
+    slot_shape_d = (owners_total, HALF + EXTRA, BLK)
+    diag, pivot, pivot_inverse, pair, col, columns = pl.pallas_call(
+        exchange_kernel,
+        in_specs=[SMEM] * 4 + whole(7) + [anywhere],
+        out_specs=whole(6),
         out_shape=[
             jax.ShapeDtypeStruct((rows, BLK, BLK), F32),
             jax.ShapeDtypeStruct((BLK, BLK), F32),
             jax.ShapeDtypeStruct((BLK, BLK), F32),
             jax.ShapeDtypeStruct((2, rows * rows, HALF, BLK), F32),
             jax.ShapeDtypeStruct((2, 2, HALF, BLK), F32),
+            jax.ShapeDtypeStruct((OWN * BLK, BLK), F32),
         ],
         scratch_shapes=[
+            VMEM(slot_shape_d, BF16),
+            VMEM(slot_shape_d, BF16),
             VMEM((tiles + 1, HALF, BLK), BF16),
-            VMEM((owners_total, HALF, BLK), BF16),
-            VMEM((owners_total, HALF, BLK), BF16),
-            VMEM((late * 2, HALF, BLK), BF16),
-            *staged(late),
-            VMEM((BLK, BLK), F32),
-            VMEM((BLK, BLK), F32),
-            VMEM((BLK, BLK), F32),
-            VMEM((BLK, BLK), F32),
-            dma((4,)),
-            dma,
-            dma,
-            dma,
+            VMEM((tiles // 2, HALF, BLK), BF16),
+            VMEM(slot_shape, BF16),
+            VMEM(slot_shape, BF16),
+            VMEM((late, order, half_width), BF16),
+            *[VMEM((BLK, BLK), F32)] * 4,
+            dma((late,)),
+            dma((late,)),
+            *[dma] * 6,
+            dma((panels - 1,)),
             dma,
             dma((panels - 1,)),
-            dma,
-            dma,
-            dma,
+            *[dma] * 3,
             dma((2,)),
             dma,
         ],
         compiler_params=pltpu.CompilerParams(
-            collective_id=2, has_side_effects=True, vmem_limit_bytes=48 * 2**20
+            collective_id=1, has_side_effects=True, vmem_limit_bytes=26 * 2**20
         ),
         cost_estimate=cost(10**10, 2**24),
-        name="second",
+        name="exchange",
     )(
-        source, pattern, diag_index, cross_index, diag_got, cross_early,
-        interface_diag.reshape(rows, BLK), hi, lo, incoming[1], w_half,
+        source, pattern, diag_index, cross_index, diag_tiles, interface_column,
+        interface_diag.reshape(rows, BLK), hi, lo, incoming, w_half, coupling,
     )
     return pl.pallas_call(
         final_kernel,
@@ -708,6 +653,7 @@
         out_specs=whole(2),
         out_shape=[jax.ShapeDtypeStruct((rows * BLK, OWN * BLK), F32)] * 2,
         scratch_shapes=[VMEM((OWN * BLK, BLK), F32)],
+        compiler_params=pltpu.CompilerParams(vmem_limit_bytes=16 * 2**20),
         cost_estimate=cost(10**9, 2**22),
         name="final",
     )(panel_s, diag, pair, col, columns, pivot, pivot_inverse)

time: 133 us -> 115 us (0.86)
  Pallas kernels: 118 us -> 105 us
  local copies, waits for them, and re-layouts: 8.48 us -> 3.9 us
    pallas_call x2 -> x1, Pallas kernels: 85.3 us -> 74 us  [per_device(): pl.pallas_call(exchange_kernel, in_specs=[SMEM] * 4 + whole(7) + [anywher...]
    slice x2 -> x0, local copies, waits for them, and re-layouts: 4.6 us -> none  [the longest x1 2.54 us: per_device(): outgoing[:EARLY]]
    unnamed x20 -> x8, local copies, waits for them, and re-layouts: 3.25 us -> 0.03 us
    dynamic_slice x0 -> x1, local copies, waits for them, and re-layouts: none -> 2.48 us  [per_device(): lax.dynamic_slice(coupling, (0, 0, (1 - upper) * half_width), (EARLY, ord...]
    ppermute x2 -> x1, starting transfers between devices: 3.53 us -> 3.02 us  [partner(): return lax.ppermute(value, 'panel', pairs)]
  transfers between devices with their start and end apart: 2 -> 1, of which waited for: 0 -> 0; matrix products, arithmetic and copies ran while one was open for 2% -> 2% of each run, Pallas kernels for 52% -> 25%
where the time goes in v3:
time: 115 us; the launch traced here: 113 us
  Pallas kernels  105 us (91%)
  local copies, waits for them, and re-layouts  3.9 us (3%)
  starting transfers between devices  3.02 us (3%)
    pallas_call x1, Pallas kernels, per_device(): pl.pallas_call(exchange_kernel, in_specs=[SMEM] * 4 + whole(7) + [anywher...  74 us
    pallas_call x1, Pallas kernels, per_device(): pl.pallas_call(solve_kernel, grid=(subs,), in_specs=[SMEM, pl.BlockSpec((...  28.4 us
    ppermute x1, starting transfers between devices, partner(): return lax.ppermute(value, 'panel', pairs)  3.02 us
    pallas_call x1, Pallas kernels, per_device(): pl.pallas_call(final_kernel, in_specs=[SMEM] + whole(6), out_specs=whole(...  2.52 us
    dynamic_slice x1, local copies, waits for them, and re-layouts, per_device(): lax.dynamic_slice(coupling, (0, 0, (1 - upper) * half_width), (EARLY, ord...  2.48 us
  transfers between devices with their start and end apart: 1, of which 0 were waited for; matrix products, arithmetic and copies ran while one was open for 2% of the time, Pallas kernels for 25%

profile of v3, /device:TPU:8, one launch (start us, length us, event | category | flops | bytes accessed | tf_op | source)
XLA Modules:
  0.0 113.2 jit_solution(15262828663434709751)
XLA Ops:
  0.6 0.0 copy-start
  0.7 2.5 %constant_dynamic-slice_fusion.1 = bf16[5,512,256]{2,1,0:T(8,128)(2,1)} fusion(bf16[8,512,512]{2,1,0:T(8,128)(2,1)} %c_any.1, s32[]{:T(128)S(6)} %select_n.46), kind=kLoop, calls=%fused_computation.20 | loop fusion | bytes 2621444 | tf_op jit(solution)/shard_map/dynamic_slice | solution.py:550
  3.1 3.0 %collective-permute-start = (bf16[5,512,256]{2,1,0:T(8,128)(2,1)}, bf16[5,512,256]{2,1,0:T(8,128)(2,1)S(1)}, u32[]{:S(2)}, u32[]{:S(2)}) collective-permute-start(bf16[5,512,256]{2,1,0:T(8,128)(2,1)} %constant_dynamic-slice_fusion.1), channel_id=1, source_target_pairs={{0,2},{1,3},{2,0},{3,1},{4,6},{5,7},{6,4},{7,5},{8,10},{9,11},{10,... | collective-permute-start | bytes 3932168 | tf_op jit(solution)/shard_map/ppermute | solution.py:533
  6.2 1.1 reshape.33
  7.2 0.1 broadcast_compare_fusion
  7.3 0.2 add_select_fusion
  7.5 0.0 copy-done
  7.6 0.1 constant_dynamic-slice_fusion
  7.6 0.1 reshape.34.pat_ref
  7.7 0.1 copy.13
  7.8 0.1 eq.25
  7.9 0.1 select_reduce_fusion
  8.0 0.2 fusion.2
  8.2 0.0 copy-start.1
  8.2 0.0 copy-start.2
  8.2 0.0 copy-start.3
  8.2 28.4 %solve.1 = (bf16[8,512,512]{2,1,0:T(8,128)(2,1)S(1)}, bf16[8,512,512]{2,1,0:T(8,128)(2,1)S(1)}, bf16[8,512,256]{2,1,0:T(8,128)(2,1)S(1)}, bf16[33,72,128]{2,1,0:T(8,128)(2,1)S(1)}) custom-call(s32[1]{0:T(128)} %bitcast.4.upper_ref, f32[8,512,512]{2,1,0:T(8,128)} %f_ref.1, bf16[8,512,512]{2,1,0:T(8,128)(2,1)} %c_any.1), custom_call_target="tpu_custom_call" | custom-call | flops 20000000000 | bytes 33554432 | tf_op jit(solution)/shard_map/solve/pallas_call | solution.py:573
  36.6 0.0 collective-permute-done.early_ref
  36.6 0.0 copy-done.1
  36.6 0.0 copy-done.2
  36.6 0.0 copy-done.3
  36.6 74.0 %exchange.1 = (f32[2,128,128]{2,1,0:T(8,128)S(1)}, f32[128,128]{1,0:T(8,128)S(1)}, f32[128,128]{1,0:T(8,128)S(1)}, f32[2,4,64,128]{3,2,1,0:T(8,128)S(1)}, f32[2,...) custom-call(s32[64]{0:T(128)S(1)} %broadcast_add_fusion.src_ref, s32[16]{0:T(128)S(1)} %reshape.34.pat_ref, ...), custom_call_target="tpu_custom_call" | custom-call | flops 10000000000 | bytes 16777216 | tf_op jit(solution)/shard_map/exchange/pallas_call | solution.py:610
  110.7 2.5 %final.1 = (f32[256,1024]{1,0:T(8,128)}, f32[256,1024]{1,0:T(8,128)}) custom-call(s32[1]{0:T(128)} %bitcast.panel_ref, f32[2,128,128]{2,1,0:T(8,128)S(1)} %get-tuple-element.16.diag_ref, f32[2,4,64,128]{3,2,1,0:T(8,128)S(1)} %get-tuple-element.17.pair_ref, f32[2,2,64,128]{3,2,1,0:T(8,128)S(1)} %get-tuple-element.18.col_ref, ...), custom_call_target="tpu_custom_call" | custom-call | flops 1000000000 | bytes 4194304 | tf_op jit(solution)/shard_map/final/pallas_call | solution.py:650
  (3 shorter events, 0.0 us)
Async XLA Ops:
  0.6 6.9 %copy-start = (s32[8,8]{1,0:T(8,128)S(1)}, s32[8,8]{1,0:T(8,128)}, u32[]{:S(2)}) copy-start(s32[8,8]{1,0:T(8,128)} %param.11) | copy-start | bytes 772
  3.1 33.4 %collective-permute-start = (bf16[5,512,256]{2,1,0:T(8,128)(2,1)}, bf16[5,512,256]{2,1,0:T(8,128)(2,1)S(1)}, u32[]{:S(2)}, u32[]{:S(2)}) collective-permute-start(bf16[5,512,256]{2,1,0:T(8,128)(2,1)} %constant_dynamic-slice_fusion.1), channel_id=1, source_target_pairs={{0,2},{1,3},{2,0},{3,1},{4,6},{5,7},{6,4},{7,5},{8,10},{9,11},{10,... | collective-permute-start | bytes 3932168 | tf_op jit(solution)/shard_map/ppermute | solution.py:533
  8.2 28.4 %copy-start.1 = (bf16[8,512,512]{2,1,0:T(8,128)(2,1)S(1)}, bf16[8,512,512]{2,1,0:T(8,128)(2,1)}, u32[]{:S(2)}) copy-start(bf16[8,512,512]{2,1,0:T(8,128)(2,1)} %c_any.1) | copy-start | bytes 12582916
  8.2 28.4 %copy-start.2 = (f32[256,128]{1,0:T(8,128)S(1)}, f32[256,128]{1,0:T(8,128)}, u32[]{:S(2)}) copy-start(f32[256,128]{1,0:T(8,128)} %icol_ref.1) | copy-start | bytes 393220
  8.2 28.4 %copy-start.3 = (f32[256]{0:T(256)S(1)}, f32[256]{0:T(256)}, u32[]{:S(2)}) copy-start(f32[256]{0:T(256)} %param.8) | copy-start | bytes 3076

commit v4 on v3

v4 whole, which is shorter than its diff:
```python
import functools

import jax
import jax.numpy as jnp
from jax import lax
from jax.experimental import pallas as pl
from jax.experimental.pallas import tpu as pltpu
from jax.sharding import PartitionSpec as P

BLK = 128
HALF = BLK // 2
OWN = 8
BASE = 32
LEVELS = 32760.0
STEP = 2
F32 = jnp.float32
BF16 = jnp.bfloat16
I16 = jnp.int16
VMEM = pltpu.VMEM


def split(x):
    hi = x.astype(BF16)
    return hi, (x - hi.astype(F32)).astype(BF16)


def mm(a, b):
    return jnp.dot(a, b, preferred_element_type=F32)


def mm_nt(a, b):
    return lax.dot_general(a, b, (((1,), (1,)), ((), ())), preferred_element_type=F32)


def mm_tn(a, b):
    return lax.dot_general(a, b, (((0,), (0,)), ((), ())), preferred_element_type=F32)


def wide(dot, a, b):
    ah, al = split(a)
    bh, bl = split(b)
    return dot(ah, bh) + (dot(ah, bl) + dot(al, bh))


def packed(a, b):
    size = b.shape[1]
    right = jnp.concatenate(split(b), axis=1)
    both = mm(jnp.concatenate(split(a), axis=1), jnp.concatenate([right, right], axis=0))
    return both[:, :size] + both[:, size:]


def to_levels(tile):
    most = jnp.max(jnp.max(jnp.abs(tile), axis=0, keepdims=True), axis=1, keepdims=True)
    level = jnp.maximum(most, 1e-30) / LEVELS
    levels = jnp.round(tile * (1.0 / level)).astype(jnp.int32).astype(I16)
    return levels, jnp.broadcast_to(level, (1, BLK))


def from_levels(levels, row):
    return levels.astype(jnp.int32).astype(F32) * row


def iota(shape, axis):
    return lax.broadcasted_iota(jnp.int32, shape, axis)


def base_inverses(f_ref, s_ref, a_ref, x_ref):
    order = f_ref.shape[1]
    subs = f_ref.shape[0] // order
    tiles = order // BLK
    per_tile = BLK // BASE
    quarter = iota((BASE, BLK), 1) // BASE

    def pick(parts, where):
        total = parts[-1]
        for q in range(per_tile - 1):
            total = jnp.where(where == q, parts[q], total)
        return total

    def gather(l, carry):
        for t in range(tiles):
            parts = [
                f_ref[
                    pl.ds(pl.multiple_of(l * order + t * BLK + q * BASE, BASE), BASE),
                    t * BLK : (t + 1) * BLK,
                ]
                for q in range(per_tile)
            ]
            start = pl.multiple_of((t * subs + l) * BASE, BASE)
            s_ref[pl.ds(start, BASE), :] = pick(parts, quarter)
        return carry

    lax.fori_loop(0, subs, gather, 0)

    def lanes(g, carry):
        rows = [
            s_ref[pl.ds(g * per_tile + k, subs * tiles, stride=BASE), :] for k in range(per_tile)
        ]
        turned = jnp.concatenate(rows, axis=0).T
        for k in range(per_tile):
            parts = [
                pltpu.roll(turned[q * BASE : (q + 1) * BASE], (q - k) * BASE % BLK, 1)
                if q != k
                else turned[q * BASE : (q + 1) * BASE]
                for q in range(per_tile)
            ]
            a_ref[g * per_tile + k] = pick(parts, quarter)
        return carry

    lax.fori_loop(0, BASE // per_tile, lanes, 0)
    rows = iota((BASE, BLK), 0)
    x_ref[...] = jnp.where(
        iota((BASE, BASE, BLK), 0) == iota((BASE, BASE, BLK), 1), 1.0, 0.0
    ).astype(F32)
    scales = [1.0 / a_ref[i, i : i + 1, :] for i in range(BASE)]
    for k in range(BASE):
        top = 8 * (k // 8 + 1)
        solved = x_ref[k, :top] * scales[k]
        x_ref[k, :top] = solved
        if k + 1 < BASE:
            x_ref[k + 1 :, :top] = x_ref[k + 1 :, :top] - a_ref[k + 1 :, k : k + 1, :] * solved[None]

    def back(g, carry):
        rows = []
        for q in range(per_tile):
            parts = [x_ref[g * per_tile + k] for k in range(per_tile)]
            parts = [
                pltpu.roll(part, (k - q) * BASE % BLK, 1) if q != k else part
                for k, part in enumerate(parts)
            ]
            rows.append(pick(parts, quarter))
        turned = jnp.concatenate(rows, axis=0).T
        for k in range(per_tile):
            s_ref[pl.ds(g * per_tile + k, subs * tiles, stride=BASE), :] = turned[
                k * BASE : (k + 1) * BASE
            ]
        return carry

    lax.fori_loop(0, BASE // per_tile, back, 0)


def full_inverses(first, count, f_ref, s_ref):
    order = f_ref.shape[1]
    subs = f_ref.shape[0] // order
    tiles = order // BLK
    row = iota((BLK, BLK), 0)
    col = iota((BLK, BLK), 1)
    quarter = iota((BASE, BLK), 1) // BASE
    where = [(first + i, t * BLK) for i in range(count) for t in range(tiles)]
    inverse = []
    for l, at in where:
        start = pl.multiple_of((at // BLK * subs + l) * BASE, BASE)
        block = s_ref[pl.ds(start, BASE), :]
        pieces = [jnp.where(quarter == q, block, 0.0) for q in range(BLK // BASE)]
        inverse.append(jnp.concatenate(pieces, axis=0))

    def rows_of(l, start, size):
        return pl.ds(pl.multiple_of(l * order + start, BASE), size)

    size = BASE
    while size < BLK:
        odd = range(size, BLK, 2 * size)
        wanted = jnp.logical_and(row // size % 2 == 1, col // size == row // size - 1)
        mask = jnp.concatenate([wanted[start : start + size] for start in odd], axis=0)
        zero = jnp.zeros((size, BLK), F32)
        strips = []
        for (l, at), known in zip(where, inverse):
            tile = jnp.concatenate(
                [f_ref[rows_of(l, at + start, size), at : at + BLK] for start in odd], axis=0
            )
            strips.append(packed(jnp.where(mask, tile, 0.0), known))
        changes = []
        for strip, known in zip(strips, inverse):
            spread, rows = [], []
            for k, start in enumerate(odd):
                spread += [zero, strip[k * size : (k + 1) * size]]
                rows.append(known[start : start + size])
            changes.append(packed(jnp.concatenate(rows, axis=0), jnp.concatenate(spread, axis=0)))
        for n, (change, known) in enumerate(zip(changes, inverse)):
            pieces = []
            for k, start in enumerate(odd):
                pieces += [
                    known[start - size : start],
                    known[start : start + size] - change[k * size : (k + 1) * size],
                ]
            inverse[n] = jnp.concatenate(pieces, axis=0)
        size *= 2
    while size < order:
        product = packed if size == BLK else functools.partial(wide, mm)
        strips = []
        for n in range(0, len(inverse), 2):
            l, at = where[n]
            below = f_ref[rows_of(l, at + size, size), at : at + size]
            strips.append(product(below, inverse[n]))
        corners = [-product(inverse[2 * n + 1], strip) for n, strip in enumerate(strips)]
        if 2 * size == order:
            return [(inverse[2 * i], corners[i], inverse[2 * i + 1]) for i in range(count)]
        zero = jnp.zeros((size, size), F32)
        inverse = [
            jnp.concatenate(
                [
                    jnp.concatenate([inverse[2 * n], zero], axis=1),
                    jnp.concatenate([corner, inverse[2 * n + 1]], axis=1),
                ],
                axis=0,
            )
            for n, corner in enumerate(corners)
        ]
        where = where[::2]
        size *= 2


def apply_inverse(hi_ref, lo_ref, l, right):
    half = hi_ref.shape[1] // 2
    top = mm(hi_ref[l, :half, :half], right[:half]) + mm(lo_ref[l, :half, :half], right[:half])
    low = mm(hi_ref[l, half:], right) + mm(lo_ref[l, half:], right)
    return jnp.concatenate([top.astype(BF16), low.astype(BF16)], axis=0)


def solve_pair(first, count, f_ref, s_ref, c_ref, hi_ref, lo_ref, w_ref, d_ref, dside_ref):
    order = hi_ref.shape[1]
    half = order // 2
    panels = lax.axis_size("panel")
    upper = lax.axis_index("panel") // (panels // 2)
    groups = c_ref.shape[2] // BLK
    row = iota((HALF, BLK), 0)
    lane = iota((HALF, BLK), 1)
    from_low = lane - HALF < row
    eye = iota((BLK, BLK), 0) == iota((BLK, BLK), 1)
    for i, blocks in enumerate(full_inverses(first, count, f_ref, s_ref)):
        for part, rows, cols in zip(blocks, (0, half, half), (0, 0, half)):
            hi, lo = split(part)
            hi_ref[first + i, rows : rows + half, cols : cols + half] = hi
            lo_ref[first + i, rows : rows + half, cols : cols + half] = lo
    for i in range(count):
        l = first + i
        solved = apply_inverse(hi_ref, lo_ref, l, c_ref[l])
        width = solved.shape[1] // 2
        w_ref[l] = jnp.where(upper == 0, solved[:, :width], solved[:, width:])
        for r in range(groups):
            block = solved[:, r * BLK : (r + 1) * BLK]
            tile = mm_tn(block, block)
            diag = jnp.sum(jnp.where(eye, tile, 0.0), axis=0, keepdims=True)
            tile = jnp.where(eye, 0.0, tile)
            folded = jnp.where(from_low, tile[HALF:], pltpu.roll(tile[:HALF], HALF, 1))
            levels, level = to_levels(folded)
            d_ref[l * groups + r] = levels
            dside_ref[l * groups + r] = jnp.concatenate([diag, level], axis=0)


MESH = pl.DeviceIdType.MESH
SUB_SHAPE = (8, 4, 2)


def sub_peer(step):
    z_total, y_total, cores = SUB_SHAPE
    me = lax.axis_index("sub")
    z, y, core = me // (y_total * cores), (me // cores) % y_total, me % cores
    m = step % z_total
    dz = z_total // 2 + (1 - 2 * (m % 2)) * ((m + 1) // 2)
    rest = step // z_total
    return (
        ((z + dz) % z_total) * y_total + (y + rest // cores) % y_total
    ) * cores + (core + rest) % cores


def all_peers(total, act):
    skip = SUB_SHAPE[0] - 1

    def one(step, carry):
        act(sub_peer(step))
        return carry

    lax.fori_loop(0, skip, one, 0)
    lax.fori_loop(skip + 1, total, one, 0)


def greet(total, panels):
    barrier = pltpu.get_barrier_semaphore()
    panel = lax.axis_index("panel")

    def signal(peer):
        pl.semaphore_signal(barrier, inc=1, device_id={"sub": peer}, device_id_type=MESH)

    all_peers(total, signal)
    for away in range(1, panels):
        pl.semaphore_signal(
            barrier, inc=1, device_id={"panel": (panel + away) % panels}, device_id_type=MESH
        )
    return lambda: pl.semaphore_wait(barrier, total - 1 + panels - 1)


def to_panel(src, dst, send, recv, away):
    panels = lax.axis_size("panel")
    peer = (lax.axis_index("panel") + away) % panels
    return pltpu.make_async_remote_copy(
        src_ref=src,
        dst_ref=dst,
        send_sem=send,
        recv_sem=recv,
        device_id={"panel": peer},
        device_id_type=MESH,
    )


def await_bytes(ref, sem):
    pltpu.make_async_copy(ref, ref, sem).wait()


def scatter_slots(total, src_ref, pairs):
    me = lax.axis_index("sub")

    def one(s, carry):
        at = src_ref[s]
        for tiles_ref, send_ref, _ in pairs:
            send_ref[s] = tiles_ref[at]
        return carry

    lax.fori_loop(0, total, one, 0, unroll=2)
    for tiles_ref, _, recv_ref in pairs:
        recv_ref[me] = tiles_ref[src_ref[me]]


def start_slots(total, pairs, send, recv):
    me = lax.axis_index("sub")

    def go(peer):
        for k, (_, send_ref, recv_ref) in enumerate(pairs):
            pltpu.make_async_remote_copy(
                src_ref=send_ref.at[peer],
                dst_ref=recv_ref.at[me],
                send_sem=send.at[k],
                recv_sem=recv.at[k],
                device_id={"sub": peer},
                device_id_type=MESH,
            ).start()

    all_peers(total, go)


def await_slots(total, pairs, send, recv):
    for k, (_, send_ref, recv_ref) in enumerate(pairs):
        await_bytes(send_ref.at[pl.ds(0, total - 1)], send.at[k])
        await_bytes(recv_ref.at[pl.ds(0, total - 1)], recv.at[k])


def cross_product(l, pat_ref, hi_ref, lo_ref, c_ref, w_ref, x_ref, xside_ref, out_ref, outside_ref, send, recv):
    panels = lax.axis_size("panel")
    upper = lax.axis_index("panel") // (panels // 2)
    low = upper == 0
    width = c_ref.shape[2] // BLK
    solved = apply_inverse(hi_ref, lo_ref, l, c_ref[l])
    for r in range(width):
        own = w_ref[l, :, r * BLK : (r + 1) * BLK]
        other = solved[:, r * BLK : (r + 1) * BLK]
        tile = mm_tn(jnp.where(low, own, other), jnp.where(low, other, own))
        tile = tile * pat_ref[l * width + r].astype(F32)
        group = l * 2 * width + width * upper + r
        levels, level = to_levels(tile)
        at = l * width + r
        x_ref[group] = jnp.where(low, levels[:HALF], levels[HALF:])
        out_ref[at] = jnp.where(low, levels[HALF:], levels[:HALF])
        xside_ref[group] = level
        outside_ref[at] = level
        to_panel(out_ref.at[at], x_ref.at[group], send.at[0], recv.at[0], panels // 2).start()
        to_panel(
            outside_ref.at[at], xside_ref.at[group], send.at[1], recv.at[1], panels // 2
        ).start()


def whole_kernel(
    src_ref, pat_ref, dindex_ref, xindex_ref, icol_ref, own_diag_ref, f_any, c_any,
    diag_ref, p_ref, inv_ref, pair_ref, col_ref, cols_ref,
    f_ref, c_ref, other_ref, hi_ref, lo_ref, w_ref, s_ref, base_ref, binv_ref,
    d_ref, dside_ref, dsend_ref, dside_send_ref, dgot_ref, dside_got_ref,
    x_ref, xside_ref, out_ref, outside_ref, xsend_ref, xside_send_ref, xgot_ref, xside_got_ref, first_ref, a_ref, b_ref, t_ref,
    local, other_send, other_recv, dslot_send, dslot_recv, slot_send, slot_recv, half_send, half_recv,
    cols_send, cols_recv, first_send, first_recv, pair_send, pair_recv, col_send, col_recv,
):
    total = lax.axis_size("sub")
    panels = lax.axis_size("panel")
    panel = lax.axis_index("panel")
    upper = panel // (panels // 2)
    subs, _, half_width = other_ref.shape
    rows = icol_ref.shape[0]
    ready = greet(total, panels)
    f_copy = pltpu.make_async_copy(f_any, f_ref, local.at[0])
    f_copy.start()
    c_copy = pltpu.make_async_copy(c_any, c_ref, local.at[1])
    c_copy.start()
    for ref in (d_ref, dside_ref, x_ref, xside_ref):
        ref[ref.shape[0] - 1] = jnp.zeros(ref.shape[1:], ref.dtype)
    d_pairs = ((d_ref, dsend_ref, dgot_ref), (dside_ref, dside_send_ref, dside_got_ref))
    x_pairs = ((x_ref, xsend_ref, xgot_ref), (xside_ref, xside_send_ref, xside_got_ref))
    ready()
    at = pl.multiple_of((1 - upper) * half_width, half_width)

    def coupling_copy(l):
        return to_panel(
            c_any.at[l, :, pl.ds(at, half_width)],
            other_ref.at[l],
            other_send.at[l],
            other_recv.at[l],
            panels // 2,
        )

    def start_coupling(l, carry):
        coupling_copy(l).start()
        return carry

    lax.fori_loop(0, subs, start_coupling, 0)
    f_copy.wait()
    base_inverses(f_ref, s_ref, base_ref, binv_ref)
    c_copy.wait()

    def solve(step, carry):
        solve_pair(step * STEP, STEP, f_ref, s_ref, c_ref, hi_ref, lo_ref, w_ref, d_ref, dside_ref)
        return carry

    lax.fori_loop(0, subs // STEP, solve, 0)
    scatter_slots(total, src_ref, d_pairs)
    start_slots(total, d_pairs, dslot_send, dslot_recv)

    def cross(l, carry):
        coupling_copy(l).wait()
        cross_product(
            l, pat_ref, hi_ref, lo_ref, other_ref, w_ref, x_ref, xside_ref, out_ref, outside_ref,
            half_send, half_recv,
        )
        return carry

    lax.fori_loop(0, subs, cross, 0)
    for k, ref in enumerate((out_ref, outside_ref)):
        await_bytes(ref, half_send.at[k])
        await_bytes(ref, half_recv.at[k])
    scatter_slots(total, src_ref, x_pairs)
    start_slots(total, x_pairs, slot_send, slot_recv)
    mine = pl.ds(pl.multiple_of(panel * rows, rows), rows)
    column_copies = [
        to_panel(icol_ref, cols_ref.at[mine], cols_send.at[away - 1], cols_recv, away)
        for away in range(1, panels)
    ]
    for copy in column_copies:
        copy.start()
    cols_ref[mine, :] = icol_ref[...]

    await_slots(total, d_pairs, dslot_send, dslot_recv)
    sum_diagonal(dindex_ref, dgot_ref, dside_got_ref, own_diag_ref, diag_ref)

    @pl.when(panel == 0)
    def _():
        first_ref[...] = diag_ref[0]
        sends = [
            to_panel(first_ref, first_ref, first_send.at[away - 1], first_recv, away)
            for away in range(1, panels)
        ]
        for copy in sends:
            copy.start()
        for copy in sends:
            copy.wait_send()

    @pl.when(panel != 0)
    def _():
        await_bytes(first_ref, first_recv)

    factor_pivot(first_ref, p_ref, inv_ref, a_ref, b_ref, t_ref)
    for copy in column_copies:
        copy.wait_send()
    await_bytes(cols_ref.at[pl.ds(0, (panels - 1) * rows)], cols_recv)
    await_slots(total, x_pairs, slot_send, slot_recv)
    sum_cross(xindex_ref, xgot_ref, xside_got_ref, pair_ref, upper)
    pair = to_panel(pair_ref.at[upper], pair_ref.at[upper], pair_send, pair_recv, panels // 2)
    pair.start()

    @pl.when(panel % 2 == 0)
    def _():
        key = pair_ref.at[upper, pl.ds(0, 2)]
        sends = [
            to_panel(key, col_ref.at[upper], col_send.at[k], col_recv, away)
            for k, away in enumerate((1, panels - 1))
        ]
        for copy in sends:
            copy.start()
        for copy in sends:
            copy.wait_send()
        pair.wait()
        col_ref[...] = pair_ref[:, :2]

    @pl.when(panel % 2 == 1)
    def _():
        pair.wait()
        await_bytes(col_ref, col_recv)


def sum_diagonal(index_ref, recv_ref, side_ref, own_diag_ref, out_ref):
    count = recv_ref.shape[0]
    places = out_ref.shape[0]

    def one(s, sums):
        side = side_ref[s]
        value = from_levels(recv_ref[s], side[1:2])
        diag = side[:1]
        at = index_ref[s]
        return tuple(
            (total + jnp.where(at == r + 1, value, 0.0), line + jnp.where(at == r + 1, diag, 0.0))
            for r, (total, line) in enumerate(sums)
        )

    start = tuple(
        (jnp.zeros((HALF, BLK), F32), own_diag_ref[r : r + 1, :]) for r in range(places)
    )
    sums = lax.fori_loop(0, count, one, start, unroll=2)
    row = iota((HALF, BLK), 0)
    lane = iota((HALF, BLK), 1)
    eye = iota((BLK, BLK), 0) == iota((BLK, BLK), 1)
    for r, (folded, diag) in enumerate(sums):
        low = jnp.where(lane - HALF < row, folded, 0.0)
        high = jnp.where(
            jnp.logical_and(lane > row, lane < HALF), pltpu.roll(folded, HALF, 1), 0.0
        )
        strict = jnp.concatenate([high, low], axis=0)
        out_ref[r] = strict + strict.T + jnp.where(eye, diag, 0.0)


def sum_cross(index_ref, recv_ref, side_ref, out_ref, slot):
    count = recv_ref.shape[0]
    places = out_ref.shape[1]

    def one(s, sums):
        value = from_levels(recv_ref[s], side_ref[s])
        at = index_ref[s]
        return tuple(
            total + jnp.where(at == r + 1, value, 0.0) for r, total in enumerate(sums)
        )

    start = tuple(jnp.zeros((HALF, BLK), F32) for _ in range(places))
    sums = lax.fori_loop(0, count, one, start, unroll=2)
    for r in range(places):
        out_ref[slot, r] = sums[r]


def factor_pivot(tile_ref, p_ref, inv_ref, a_ref, b_ref, t_ref):
    step = 8
    a_ref[...] = tile_ref[...]
    b_ref[...] = jnp.where(iota((BLK, BLK), 0) == iota((BLK, BLK), 1), 1.0, 0.0)
    row = iota((BLK, BLK), 0)
    sub = iota((step, BLK), 0)
    lane = iota((step, BLK), 1)

    def group(g, carry):
        at = pl.ds(pl.multiple_of(g * step, step), step)
        a, b = a_ref[...], b_ref[...]
        rows, right = a_ref[at, :], b_ref[at, :]
        factor_rows, inverse_rows = [], []
        for s in range(step):
            pivot_row, right_row = rows[s : s + 1], right[s : s + 1]
            pivot = jnp.broadcast_to(pivot_row[:, s : s + 1], (1, BLK))
            root = 1.0 / jnp.sqrt(pivot)
            inverse = 1.0 / pivot
            factor_rows.append(pivot_row * root)
            inverse_rows.append(right_row * root)
            scaled, right_scaled = pivot_row * inverse, right_row * inverse
            near = jnp.where(sub > s, rows[:, s : s + 1], 0.0)
            far = jnp.where(row > g * step + s, a[:, s : s + 1], 0.0)
            rows, right = rows - near * scaled, right - near * right_scaled
            a, b = a - far * scaled, b - far * right_scaled
        a_ref[...] = pltpu.roll(a, BLK - step, 1)
        b_ref[...] = b
        block = jnp.concatenate(factor_rows, axis=0)
        block = jnp.where(jnp.logical_and(lane >= sub, lane < BLK - g * step), block, 0.0)
        t_ref[at, :] = pltpu.roll(block, g * step, 1)
        inv_ref[at, :] = jnp.concatenate(inverse_rows, axis=0)
        return carry

    lax.fori_loop(0, BLK // step, group, 0)
    p_ref[...] = t_ref[...].T


def final_kernel(panel_ref, diag_ref, pair_ref, col_ref, icol_ref, p_ref, inv_ref, asm_ref, fac_ref, l_ref):
    panel = panel_ref[0]
    lower = panel < 2
    other = (panel + 2) % 4
    asm_ref[...] = jnp.zeros_like(asm_ref)
    for r in range(2):
        at = pl.multiple_of((panel * 2 + r) * BLK, BLK)
        asm_ref[r * BLK : (r + 1) * BLK, pl.ds(at, BLK)] = diag_ref[r]
    for a in range(2):
        for b in range(2):
            tile = jnp.concatenate([pair_ref[0, a * 2 + b], pair_ref[1, a * 2 + b]], axis=0)
            tile = jnp.where(lower, tile, tile.T)
            row = pl.multiple_of(jnp.where(lower, a, b) * BLK, BLK)
            at = pl.multiple_of((other * 2 + jnp.where(lower, b, a)) * BLK, BLK)
            asm_ref[pl.ds(row, BLK), pl.ds(at, BLK)] = tile
    own = pl.multiple_of(panel * 2 * BLK, BLK)
    off = jnp.logical_or(panel > 0, iota((2 * BLK, BLK), 0) >= BLK)
    asm_ref[:, :BLK] = asm_ref[:, :BLK] + jnp.where(off, icol_ref[pl.ds(own, 2 * BLK), :], 0.0)
    inv_hi, inv_lo = split(inv_ref[...])
    l_ref[:BLK, :] = p_ref[...]
    for r in range(1, OWN):
        key = icol_ref[r * BLK : (r + 1) * BLK, :]
        if r in (4, 5):
            key = key + jnp.concatenate([col_ref[0, r - 4], col_ref[1, r - 4]], axis=0).T
        kh, kl = split(key)
        l_ref[r * BLK : (r + 1) * BLK, :] = mm_nt(kh, inv_hi) + (
            mm_nt(kh, inv_lo) + mm_nt(kl, inv_hi)
        )
    mine = l_ref[pl.ds(own, 2 * BLK), :]
    mh, ml = split(mine)
    fac_ref[:, :BLK] = mine
    for c in range(1, OWN):
        lh, ll = split(l_ref[c * BLK : (c + 1) * BLK, :])
        update = mm_nt(mh, lh) + (mm_nt(mh, ll) + mm_nt(ml, lh))
        fac_ref[:, c * BLK : (c + 1) * BLK] = asm_ref[:, c * BLK : (c + 1) * BLK] - jnp.where(
            off, update, 0.0
        )


def cost(flops, nbytes):
    return pl.CostEstimate(flops=flops, bytes_accessed=nbytes, transcendentals=0)


def whole(count):
    return [pl.BlockSpec(memory_space=VMEM)] * count


SMEM = pl.BlockSpec(memory_space=pltpu.SMEM)


def per_device(
    interior_factor, coupling, interface_diag, interface_column, block_map, pair_pattern
):
    subs, order, width = coupling.shape
    owners_total = lax.axis_size("sub")
    panels = lax.axis_size("panel")
    sub = lax.axis_index("sub")
    panel = lax.axis_index("panel")
    upper = (panel >= panels // 2).astype(jnp.int32)
    panel_s = panel.astype(jnp.int32).reshape(1)
    groups = width // BLK
    half_width = width // 2

    maps = block_map.reshape(owners_total, subs, panels, groups)
    owner = maps[:, :, 0, :] // OWN
    match = (owner == sub).astype(jnp.int32)
    place = maps % 2
    base = panel % 2
    own_place = lax.dynamic_index_in_dim(place, panel, 2, keepdims=False)
    low_place = lax.dynamic_index_in_dim(place, base, 2, keepdims=False)
    high_place = lax.dynamic_index_in_dim(place, base + 2, 2, keepdims=False)
    diag_index = jnp.sum(match * (1 + own_place), axis=(1, 2))
    cross_index = jnp.sum(match * (1 + 2 * low_place + high_place), axis=(1, 2))
    slots = lax.dynamic_index_in_dim(owner, sub, 0, keepdims=False).reshape(-1)
    tiles = subs * groups
    filled = (slots[None, :] == jnp.arange(owners_total, dtype=jnp.int32)[:, None]).astype(jnp.int32)
    source = tiles + jnp.sum(
        filled * (jnp.arange(tiles, dtype=jnp.int32) - tiles)[None, :], axis=1
    )
    pattern = lax.dynamic_slice_in_dim(pair_pattern, base * groups + upper * 2, 2, 1).reshape(-1)

    anywhere = pl.BlockSpec(memory_space=pl.ANY)
    dma = pltpu.SemaphoreType.DMA

    rows = OWN // panels
    diag, pivot, pivot_inverse, pair, col, columns = pl.pallas_call(
        whole_kernel,
        in_specs=[SMEM] * 4 + whole(2) + [anywhere] * 2,
        out_specs=whole(6),
        out_shape=[
            jax.ShapeDtypeStruct((rows, BLK, BLK), F32),
            jax.ShapeDtypeStruct((BLK, BLK), F32),
            jax.ShapeDtypeStruct((BLK, BLK), F32),
            jax.ShapeDtypeStruct((2, rows * rows, HALF, BLK), F32),
            jax.ShapeDtypeStruct((2, 2, HALF, BLK), F32),
            jax.ShapeDtypeStruct((OWN * BLK, BLK), F32),
        ],
        scratch_shapes=[
            VMEM((subs * order, order), F32),
            VMEM((subs, order, width), BF16),
            VMEM((subs, order, half_width), BF16),
            VMEM((subs, order, order), BF16),
            VMEM((subs, order, order), BF16),
            VMEM((subs, order, half_width), BF16),
            VMEM((subs * order // BLK * BASE, BLK), F32),
            VMEM((BASE, BASE, BLK), F32),
            VMEM((BASE, BASE, BLK), F32),
            VMEM((tiles + 1, HALF, BLK), I16),
            VMEM((tiles + 1, 2, BLK), F32),
            VMEM((owners_total, HALF, BLK), I16),
            VMEM((owners_total, 2, BLK), F32),
            VMEM((owners_total, HALF, BLK), I16),
            VMEM((owners_total, 2, BLK), F32),
            VMEM((tiles + 1, HALF, BLK), I16),
            VMEM((tiles + 1, 1, BLK), F32),
            VMEM((tiles // 2, HALF, BLK), I16),
            VMEM((tiles // 2, 1, BLK), F32),
            VMEM((owners_total, HALF, BLK), I16),
            VMEM((owners_total, 1, BLK), F32),
            VMEM((owners_total, HALF, BLK), I16),
            VMEM((owners_total, 1, BLK), F32),
            *[VMEM((BLK, BLK), F32)] * 4,
            dma((2,)),
            dma((subs,)),
            dma((subs,)),
            *[dma((2,))] * 6,
            dma((panels - 1,)),
            dma,
            dma((panels - 1,)),
            *[dma] * 3,
            dma((2,)),
            dma,
        ],
        compiler_params=pltpu.CompilerParams(
            collective_id=1, has_side_effects=True, vmem_limit_bytes=50 * 2**20
        ),
        cost_estimate=cost(10**10, 2**24),
        name="whole",
    )(
        source, pattern, diag_index, cross_index, interface_column,
        interface_diag.reshape(rows, BLK), interior_factor.reshape(subs * order, order), coupling,
    )
    return pl.pallas_call(
        final_kernel,
        in_specs=[SMEM] + whole(6),
        out_specs=whole(2),
        out_shape=[jax.ShapeDtypeStruct((rows * BLK, OWN * BLK), F32)] * 2,
        scratch_shapes=[VMEM((OWN * BLK, BLK), F32)],
        compiler_params=pltpu.CompilerParams(vmem_limit_bytes=16 * 2**20),
        cost_estimate=cost(10**9, 2**22),
        name="final",
    )(panel_s, diag, pair, col, columns, pivot, pivot_inverse)


def solution(mesh):
    return jax.shard_map(
        per_device,
        mesh=mesh,
        in_specs=(
            P("sub", None, None),
            P("sub", None, "panel"),
            P(("sub", "panel")),
            P(("sub", "panel"), None),
            P(),
            P("sub", None),
        ),
        out_specs=(P(("sub", "panel"), None), P(("sub", "panel"), None)),
        check_vma=False,
    )
```

time: 115 us -> 107 us (0.930)
  Pallas kernels: 105 us -> 101 us
  starting transfers between devices: 3.02 us -> 0 us
    pallas_call x2 -> x1, Pallas kernels: 102 us -> 98.5 us  [per_device(): pl.pallas_call(whole_kernel, in_specs=[SMEM] * 4 + whole(2) + [anywhere]...]
    ppermute x1 -> x0, starting transfers between devices: 3.02 us -> none  [partner(): return lax.ppermute(value, 'panel', pairs)]
    dynamic_slice x1 -> x0, local copies, waits for them, and re-layouts: 2.48 us -> none  [per_device(): lax.dynamic_slice(coupling, (0, 0, (1 - upper) * half_width), (EARLY, ord...]
    unnamed x8 -> x6, local copies, waits for them, and re-layouts: 0.03 us -> 2.23 us
  transfers between devices with their start and end apart: 1 -> 0, of which waited for: 0 -> 0; matrix products, arithmetic and copies ran while one was open for 2% -> 0% of each run, Pallas kernels for 25% -> 0%
where the time goes in v4:
time: 107 us; the launch traced here: 106 us
  Pallas kernels  101 us (94%)
  local copies, waits for them, and re-layouts  3.62 us (3%)
    pallas_call x1, Pallas kernels, per_device(): pl.pallas_call(whole_kernel, in_specs=[SMEM] * 4 + whole(2) + [anywhere]...  98.5 us
    pallas_call x1, Pallas kernels, per_device(): pl.pallas_call(final_kernel, in_specs=[SMEM] + whole(6), out_specs=whole(...  2.51 us
    unnamed x6, local copies, waits for them, and re-layouts  2.23 us

profile of v4, /device:TPU:8, one launch (start us, length us, event | category | flops | bytes accessed | tf_op | source)
XLA Modules:
  0.0 105.9 jit_solution(9057002633696727681)
XLA Ops:
  0.6 0.0 copy-start
  0.7 0.6 copy-done
  1.3 0.1 constant_dynamic-slice_fusion
  1.4 0.1 reshape.34.pat_ref
  1.5 1.1 %reshape.33 = s32[64,8,4,4]{1,0,3,2:T(8,128)S(1)} reshape(s32[512,16]{0,1:T(8,128)} %param.10) | data formatting | bytes 65536 | tf_op jit(solution)/shard_map/reshape | solution.py:642
  2.5 0.1 broadcast_compare_fusion
  2.7 0.2 add_select_fusion
  2.9 0.2 fusion.2
  3.0 0.1 copy.13
  3.1 0.1 eq.25
  3.2 0.1 select_reduce_fusion
  3.3 0.0 copy-start.1
  3.3 0.9 copy-done.1
  4.2 0.0 copy-start.2
  4.2 0.7 copy-done.2
  4.9 98.5 %whole.1 = (f32[2,128,128]{2,1,0:T(8,128)S(1)}, f32[128,128]{1,0:T(8,128)S(1)}, f32[128,128]{1,0:T(8,128)S(1)}, f32[2,4,64,128]{3,2,1,0:T(8,128)S(1)}, f32[2,2,6...) custom-call(s32[64]{0:T(128)S(1)} %broadcast_add_fusion.src_ref, s32[16]{0:T(128)S(1)} %reshape.34.pat_ref, ...), custom_call_target="tpu_custom_call" | custom-call | flops 10000000000 | bytes 16777216 | tf_op jit(solution)/shard_map/whole/pallas_call | solution.py:664
  103.4 2.5 %final.1 = (f32[256,1024]{1,0:T(8,128)}, f32[256,1024]{1,0:T(8,128)}) custom-call(s32[1]{0:T(128)} %bitcast.panel_ref, f32[2,128,128]{2,1,0:T(8,128)S(1)} %get-tuple-element.8.diag_ref, f32[2,4,64,128]{3,2,1,0:T(8,128)S(1)} %get-tuple-element.9.pair_ref, f32[2,2,64,128]{3,2,1,0:T(8,128)S(1)} %get-tuple-element.10.col_ref, ...), custom_call_target="tpu_custom_call" | custom-call | flops 1000000000 | bytes 4194304 | tf_op jit(solution)/shard_map/final/pallas_call | solution.py:721
  (3 shorter events, 0.0 us)
Async XLA Ops:
  0.6 0.7 copy-start
  3.3 0.9 copy-start.1
  4.2 0.7 copy-start.2

commit v5 on v4

--- a/solution.py
+++ b/solution.py
@@ -12,6 +12,7 @@
 OWN = 8
 BASE = 32
 LEVELS = 32760.0
+AHEAD = 3
 STEP = 2
 F32 = jnp.float32
 BF16 = jnp.bfloat16
@@ -344,36 +345,59 @@
         await_bytes(recv_ref.at[pl.ds(0, total - 1)], recv.at[k])
 
 
-def cross_product(l, pat_ref, hi_ref, lo_ref, c_ref, w_ref, x_ref, xside_ref, out_ref, outside_ref, send, recv):
+def pack_columns(phase, left, right):
+    left, right = left.astype(F32), right.astype(F32)
+    low = iota(left.shape, 1) < HALF
+    if phase == 0:
+        return jnp.where(low, left, pltpu.roll(right, HALF, 1)).astype(BF16)
+    return jnp.where(low, pltpu.roll(left, HALF, 1), right).astype(BF16)
+
+
+def cross_product(phase, l, pat_ref, hi_ref, lo_ref, c_ref, w_ref, x_refs, xside_refs, out_ref, outside_ref, send, recv):
     panels = lax.axis_size("panel")
     upper = lax.axis_index("panel") // (panels // 2)
-    low = upper == 0
-    width = c_ref.shape[2] // BLK
-    solved = apply_inverse(hi_ref, lo_ref, l, c_ref[l])
+    stay_low = upper == phase
+    width = w_ref.shape[2] // BLK
+    solved = apply_inverse(hi_ref, lo_ref, l, c_ref[phase, l])
+    low = iota((BLK, BLK), 1) < HALF
+    narrow = iota((HALF // 2, BLK), 1) < HALF
     for r in range(width):
-        own = w_ref[l, :, r * BLK : (r + 1) * BLK]
-        other = solved[:, r * BLK : (r + 1) * BLK]
-        tile = mm_tn(jnp.where(low, own, other), jnp.where(low, other, own))
+        tile = mm_tn(w_ref[l, :, r * BLK : (r + 1) * BLK], solved)
         tile = tile * pat_ref[l * width + r].astype(F32)
+        tile = jnp.where(low, tile, 0.0) if r == 0 else jnp.where(low, 0.0, tile)
+        quarters = []
+        for half in range(2):
+            top = tile[half * HALF : half * HALF + HALF // 2]
+            bottom = tile[half * HALF + HALF // 2 : (half + 1) * HALF]
+            if r == 0:
+                bottom = pltpu.roll(bottom, HALF, 1)
+            else:
+                top = pltpu.roll(top, HALF, 1)
+            quarters.append(jnp.where(narrow, top, bottom))
+        levels, level = to_levels(jnp.concatenate(quarters, axis=0))
+        first, second = levels[: HALF // 2], levels[HALF // 2 :]
         group = l * 2 * width + width * upper + r
-        levels, level = to_levels(tile)
         at = l * width + r
-        x_ref[group] = jnp.where(low, levels[:HALF], levels[HALF:])
-        out_ref[at] = jnp.where(low, levels[HALF:], levels[:HALF])
-        xside_ref[group] = level
-        outside_ref[at] = level
-        to_panel(out_ref.at[at], x_ref.at[group], send.at[0], recv.at[0], panels // 2).start()
+        x_refs[phase][group] = jnp.where(stay_low, first, second)
+        out_ref[phase, at] = jnp.where(stay_low, second, first)
+        xside_refs[phase][group] = level
+        outside_ref[phase, at] = level
         to_panel(
-            outside_ref.at[at], xside_ref.at[group], send.at[1], recv.at[1], panels // 2
+            out_ref.at[phase, at], x_refs[phase].at[group],
+            send.at[2 * phase], recv.at[2 * phase], panels // 2,
+        ).start()
+        to_panel(
+            outside_ref.at[phase, at], xside_refs[phase].at[group],
+            send.at[2 * phase + 1], recv.at[2 * phase + 1], panels // 2,
         ).start()
 
 
 def whole_kernel(
     src_ref, pat_ref, dindex_ref, xindex_ref, icol_ref, own_diag_ref, f_any, c_any,
     diag_ref, p_ref, inv_ref, pair_ref, col_ref, cols_ref,
-    f_ref, c_ref, other_ref, hi_ref, lo_ref, w_ref, s_ref, base_ref, binv_ref,
+    f_ref, c_ref, give_ref, other_ref, hi_ref, lo_ref, w_ref, s_ref, base_ref, binv_ref,
     d_ref, dside_ref, dsend_ref, dside_send_ref, dgot_ref, dside_got_ref,
-    x_ref, xside_ref, out_ref, outside_ref, xsend_ref, xside_send_ref, xgot_ref, xside_got_ref, first_ref, a_ref, b_ref, t_ref,
+    x0_ref, x1_ref, xside0_ref, xside1_ref, out_ref, outside_ref, xsend_ref, xside_send_ref, xgot_ref, xside_got_ref, part_ref, first_ref, a_ref, b_ref, t_ref,
     local, other_send, other_recv, dslot_send, dslot_recv, slot_send, slot_recv, half_send, half_recv,
     cols_send, cols_recv, first_send, first_recv, pair_send, pair_recv, col_send, col_recv,
 ):
@@ -381,37 +405,56 @@
     panels = lax.axis_size("panel")
     panel = lax.axis_index("panel")
     upper = panel // (panels // 2)
-    subs, _, half_width = other_ref.shape
+    subs = c_ref.shape[0]
     rows = icol_ref.shape[0]
     ready = greet(total, panels)
+    c_copy = pltpu.make_async_copy(c_any, c_ref, local.at[1])
+    c_copy.start()
     f_copy = pltpu.make_async_copy(f_any, f_ref, local.at[0])
     f_copy.start()
-    c_copy = pltpu.make_async_copy(c_any, c_ref, local.at[1])
-    c_copy.start()
-    for ref in (d_ref, dside_ref, x_ref, xside_ref):
+    x_refs, xside_refs = (x0_ref, x1_ref), (xside0_ref, xside1_ref)
+    for ref in (d_ref, dside_ref, *x_refs, *xside_refs):
         ref[ref.shape[0] - 1] = jnp.zeros(ref.shape[1:], ref.dtype)
     d_pairs = ((d_ref, dsend_ref, dgot_ref), (dside_ref, dside_send_ref, dside_got_ref))
-    x_pairs = ((x_ref, xsend_ref, xgot_ref), (xside_ref, xside_send_ref, xside_got_ref))
+    x_pairs = [
+        (
+            (x_refs[phase], xsend_ref.at[phase], xgot_ref.at[phase]),
+            (xside_refs[phase], xside_send_ref.at[phase], xside_got_ref.at[phase]),
+        )
+        for phase in range(2)
+    ]
+    c_copy.wait()
+
+    def give(l, carry):
+        cols = c_ref[l]
+        cols = jnp.where(upper == 0, cols[:, 2 * BLK :], cols[:, : 2 * BLK])
+        for phase in range(2):
+            give_ref[phase, l] = pack_columns(phase, cols[:, :BLK], cols[:, BLK:])
+        return carry
+
+    lax.fori_loop(0, subs, give, 0)
     ready()
-    at = pl.multiple_of((1 - upper) * half_width, half_width)
-
-    def coupling_copy(l):
+
+    def coupling_copy(phase, l):
         return to_panel(
-            c_any.at[l, :, pl.ds(at, half_width)],
-            other_ref.at[l],
-            other_send.at[l],
-            other_recv.at[l],
+            give_ref.at[phase, l],
+            other_ref.at[phase, l],
+            other_send.at[phase, l],
+            other_recv.at[phase, l],
             panels // 2,
         )
 
-    def start_coupling(l, carry):
-        coupling_copy(l).start()
-        return carry
-
-    lax.fori_loop(0, subs, start_coupling, 0)
+    def start_coupling(phase, first, last):
+        def one(l, carry):
+            coupling_copy(phase, l).start()
+            return carry
+
+        lax.fori_loop(first, last, one, 0)
+
+    start_coupling(0, 0, subs)
+    start_coupling(1, 0, AHEAD)
     f_copy.wait()
     base_inverses(f_ref, s_ref, base_ref, binv_ref)
-    c_copy.wait()
 
     def solve(step, carry):
         solve_pair(step * STEP, STEP, f_ref, s_ref, c_ref, hi_ref, lo_ref, w_ref, d_ref, dside_ref)
@@ -421,20 +464,36 @@
     scatter_slots(total, src_ref, d_pairs)
     start_slots(total, d_pairs, dslot_send, dslot_recv)
 
-    def cross(l, carry):
-        coupling_copy(l).wait()
+    def cross(phase, l):
+        coupling_copy(phase, l).wait()
         cross_product(
-            l, pat_ref, hi_ref, lo_ref, other_ref, w_ref, x_ref, xside_ref, out_ref, outside_ref,
-            half_send, half_recv,
+            phase, l, pat_ref, hi_ref, lo_ref, other_ref, w_ref, x_refs, xside_refs, out_ref,
+            outside_ref, half_send, half_recv,
         )
+
+    def cross_first(l, carry):
+        cross(0, l)
+        coupling_copy(1, l + AHEAD).start()
         return carry
 
-    lax.fori_loop(0, subs, cross, 0)
-    for k, ref in enumerate((out_ref, outside_ref)):
-        await_bytes(ref, half_send.at[k])
-        await_bytes(ref, half_recv.at[k])
-    scatter_slots(total, src_ref, x_pairs)
-    start_slots(total, x_pairs, slot_send, slot_recv)
+    def cross_rest(phase):
+        def one(l, carry):
+            cross(phase, l)
+            return carry
+
+        return one
+
+    for phase in range(2):
+        if phase == 0:
+            lax.fori_loop(0, subs - AHEAD, cross_first, 0)
+            lax.fori_loop(subs - AHEAD, subs, cross_rest(0), 0)
+        else:
+            lax.fori_loop(0, subs, cross_rest(1), 0)
+        for k, ref in enumerate((out_ref, outside_ref)):
+            await_bytes(ref.at[phase], half_send.at[2 * phase + k])
+            await_bytes(ref.at[phase], half_recv.at[2 * phase + k])
+        scatter_slots(total, src_ref, x_pairs[phase])
+        start_slots(total, x_pairs[phase], slot_send.at[phase], slot_recv.at[phase])
     mine = pl.ds(pl.multiple_of(panel * rows, rows), rows)
     column_copies = [
         to_panel(icol_ref, cols_ref.at[mine], cols_send.at[away - 1], cols_recv, away)
@@ -467,8 +526,10 @@
     for copy in column_copies:
         copy.wait_send()
     await_bytes(cols_ref.at[pl.ds(0, (panels - 1) * rows)], cols_recv)
-    await_slots(total, x_pairs, slot_send, slot_recv)
-    sum_cross(xindex_ref, xgot_ref, xside_got_ref, pair_ref, upper)
+    for phase in range(2):
+        await_slots(total, x_pairs[phase], slot_send.at[phase], slot_recv.at[phase])
+        sum_cross(xindex_ref, xgot_ref.at[phase], xside_got_ref.at[phase], part_ref.at[phase])
+    join_parts(part_ref, pair_ref, upper)
     pair = to_panel(pair_ref.at[upper], pair_ref.at[upper], pair_send, pair_recv, panels // 2)
     pair.start()
 
@@ -522,9 +583,9 @@
         out_ref[r] = strict + strict.T + jnp.where(eye, diag, 0.0)
 
 
-def sum_cross(index_ref, recv_ref, side_ref, out_ref, slot):
-    count = recv_ref.shape[0]
-    places = out_ref.shape[1]
+def sum_cross(index_ref, recv_ref, side_ref, out_ref):
+    count, height, _ = recv_ref.shape
+    places = out_ref.shape[0]
 
     def one(s, sums):
         value = from_levels(recv_ref[s], side_ref[s])
@@ -533,10 +594,36 @@
             total + jnp.where(at == r + 1, value, 0.0) for r, total in enumerate(sums)
         )
 
-    start = tuple(jnp.zeros((HALF, BLK), F32) for _ in range(places))
+    start = tuple(jnp.zeros((height, BLK), F32) for _ in range(places))
     sums = lax.fori_loop(0, count, one, start, unroll=2)
     for r in range(places):
-        out_ref[slot, r] = sums[r]
+        out_ref[r] = sums[r]
+
+
+def join_parts(part_ref, out_ref, upper):
+    places = out_ref.shape[1]
+    low = iota((HALF, BLK), 1) < HALF
+
+    def at_low(part):
+        return jnp.concatenate([part, pltpu.roll(part, HALF, 1)], axis=0)
+
+    def at_high(part):
+        return jnp.concatenate([pltpu.roll(part, HALF, 1), part], axis=0)
+
+    for r in range(places):
+        zero, one = part_ref[0, r], part_ref[1, r]
+        left, right = jnp.where(upper == 0, zero, one), jnp.where(upper == 0, one, zero)
+        straight = jnp.where(low, at_low(left), at_high(right))
+        turned = jnp.concatenate(
+            [at_low(part_ref[0, places + r]), at_low(part_ref[1, places + r])], axis=0
+        ).T[:HALF]
+        out_ref[upper, r] = straight + turned
+
+
+def join_pair(first, second):
+    low = iota((HALF, BLK), 1) < HALF
+    second = pltpu.roll(second, HALF, 1)
+    return jnp.concatenate([jnp.where(low, first, second), jnp.where(low, second, first)], axis=0)
 
 
 def factor_pivot(tile_ref, p_ref, inv_ref, a_ref, b_ref, t_ref):
@@ -586,7 +673,7 @@
         asm_ref[r * BLK : (r + 1) * BLK, pl.ds(at, BLK)] = diag_ref[r]
     for a in range(2):
         for b in range(2):
-            tile = jnp.concatenate([pair_ref[0, a * 2 + b], pair_ref[1, a * 2 + b]], axis=0)
+            tile = join_pair(pair_ref[0, a * 2 + b], pair_ref[1, a * 2 + b])
             tile = jnp.where(lower, tile, tile.T)
             row = pl.multiple_of(jnp.where(lower, a, b) * BLK, BLK)
             at = pl.multiple_of((other * 2 + jnp.where(lower, b, a)) * BLK, BLK)
@@ -599,7 +686,7 @@
     for r in range(1, OWN):
         key = icol_ref[r * BLK : (r + 1) * BLK, :]
         if r in (4, 5):
-            key = key + jnp.concatenate([col_ref[0, r - 4], col_ref[1, r - 4]], axis=0).T
+            key = key + join_pair(col_ref[0, r - 4], col_ref[1, r - 4]).T
         kh, kl = split(key)
         l_ref[r * BLK : (r + 1) * BLK, :] = mm_nt(kh, inv_hi) + (
             mm_nt(kh, inv_lo) + mm_nt(kl, inv_hi)
@@ -648,7 +735,10 @@
     low_place = lax.dynamic_index_in_dim(place, base, 2, keepdims=False)
     high_place = lax.dynamic_index_in_dim(place, base + 2, 2, keepdims=False)
     diag_index = jnp.sum(match * (1 + own_place), axis=(1, 2))
-    cross_index = jnp.sum(match * (1 + 2 * low_place + high_place), axis=(1, 2))
+    by_upper = (jnp.arange(groups, dtype=jnp.int32) >= groups // 2).astype(jnp.int32)
+    cross_index = jnp.sum(
+        match * (1 + 2 * low_place + high_place + 4 * by_upper[None, None, :]), axis=(1, 2)
+    )
     slots = lax.dynamic_index_in_dim(owner, sub, 0, keepdims=False).reshape(-1)
     tiles = subs * groups
     filled = (slots[None, :] == jnp.arange(owners_total, dtype=jnp.int32)[:, None]).astype(jnp.int32)
@@ -676,7 +766,8 @@
         scratch_shapes=[
             VMEM((subs * order, order), F32),
             VMEM((subs, order, width), BF16),
-            VMEM((subs, order, half_width), BF16),
+            VMEM((2, subs, order, BLK), BF16),
+            VMEM((2, subs, order, BLK), BF16),
             VMEM((subs, order, order), BF16),
             VMEM((subs, order, order), BF16),
             VMEM((subs, order, half_width), BF16),
@@ -689,19 +780,22 @@
             VMEM((owners_total, 2, BLK), F32),
             VMEM((owners_total, HALF, BLK), I16),
             VMEM((owners_total, 2, BLK), F32),
-            VMEM((tiles + 1, HALF, BLK), I16),
-            VMEM((tiles + 1, 1, BLK), F32),
-            VMEM((tiles // 2, HALF, BLK), I16),
-            VMEM((tiles // 2, 1, BLK), F32),
-            VMEM((owners_total, HALF, BLK), I16),
-            VMEM((owners_total, 1, BLK), F32),
-            VMEM((owners_total, HALF, BLK), I16),
-            VMEM((owners_total, 1, BLK), F32),
+            *[VMEM((tiles + 1, HALF // 2, BLK), I16)] * 2,
+            *[VMEM((tiles + 1, 1, BLK), F32)] * 2,
+            VMEM((2, tiles // 2, HALF // 2, BLK), I16),
+            VMEM((2, tiles // 2, 1, BLK), F32),
+            VMEM((2, owners_total, HALF // 2, BLK), I16),
+            VMEM((2, owners_total, 1, BLK), F32),
+            VMEM((2, owners_total, HALF // 2, BLK), I16),
+            VMEM((2, owners_total, 1, BLK), F32),
+            VMEM((2, 2 * rows * rows, HALF // 2, BLK), F32),
             *[VMEM((BLK, BLK), F32)] * 4,
             dma((2,)),
-            dma((subs,)),
-            dma((subs,)),
-            *[dma((2,))] * 6,
+            dma((2, subs)),
+            dma((2, subs)),
+            *[dma((2,))] * 2,
+            *[dma((2, 2))] * 2,
+            *[dma((4,))] * 2,
             dma((panels - 1,)),
             dma,
             dma((panels - 1,)),

time: 107 us -> 118 us (1.10)
  Pallas kernels: 101 us -> 112 us
    pallas_call x1, Pallas kernels: 98.5 us -> 110 us  [per_device(): pl.pallas_call(whole_kernel, in_specs=[SMEM] * 4 + whole(2) + [anywhere]...]
where the time goes in v5:
time: 118 us; the launch traced here: 117 us
  Pallas kernels  112 us (95%)
  local copies, waits for them, and re-layouts  3.6 us (3%)
    pallas_call x1, Pallas kernels, per_device(): pl.pallas_call(whole_kernel, in_specs=[SMEM] * 4 + whole(2) + [anywhere]...  110 us
    pallas_call x1, Pallas kernels, per_device(): pl.pallas_call(final_kernel, in_specs=[SMEM] + whole(6), out_specs=whole(...  2.41 us

profile of v5, /device:TPU:8, one launch (start us, length us, event | category | flops | bytes accessed | tf_op | source)
XLA Modules:
  0.0 117.4 jit_solution(16707606713380011937)
XLA Ops:
  0.6 0.0 copy-start
  0.7 0.6 copy-done
  1.3 0.1 constant_dynamic-slice_fusion
  1.4 0.1 reshape.40.pat_ref
  1.5 1.1 reshape.39
  2.5 0.1 broadcast_compare_fusion
  2.7 0.2 add_select_fusion
  2.9 0.2 fusion.3
  3.1 0.1 copy.13
  3.1 0.1 eq.25
  3.2 0.1 select_reduce_fusion
  3.3 0.0 copy-start.1
  3.3 0.9 copy-done.1
  4.2 0.0 copy-start.2
  4.2 0.7 copy-done.2
  4.9 110.1 %whole.1 = (f32[2,128,128]{2,1,0:T(8,128)S(1)}, f32[128,128]{1,0:T(8,128)S(1)}, f32[128,128]{1,0:T(8,128)S(1)}, f32[2,4,64,128]{3,2,1,0:T(8,128)S(1)}, f32[2,2,6...) custom-call(s32[64]{0:T(128)S(1)} %broadcast_add_fusion.src_ref, s32[16]{0:T(128)S(1)} %reshape.40.pat_ref, ...), custom_call_target="tpu_custom_call" | custom-call | flops 10000000000 | bytes 16777216 | tf_op jit(solution)/shard_map/whole/pallas_call | solution.py:754
  115.0 2.4 %final.1 = (f32[256,1024]{1,0:T(8,128)}, f32[256,1024]{1,0:T(8,128)}) custom-call(s32[1]{0:T(128)} %bitcast.panel_ref, f32[2,128,128]{2,1,0:T(8,128)S(1)} %get-tuple-element.8.diag_ref, f32[2,4,64,128]{3,2,1,0:T(8,128)S(1)} %get-tuple-element.9.pair_ref, f32[2,2,64,128]{3,2,1,0:T(8,128)S(1)} %get-tuple-element.10.col_ref, ...), custom_call_target="tpu_custom_call" | custom-call | flops 1000000000 | bytes 4194304 | tf_op jit(solution)/shard_map/final/pallas_call | solution.py:815
  (4 shorter events, 0.0 us)
Async XLA Ops:
  0.6 0.7 copy-start
  3.3 0.9 copy-start.1
  4.2 0.7 copy-start.2

commit v6 on v4

--- a/solution.py
+++ b/solution.py
@@ -316,7 +316,7 @@
             send_ref[s] = tiles_ref[at]
         return carry
 
-    lax.fori_loop(0, total, one, 0, unroll=2)
+    lax.fori_loop(0, total, one, 0, unroll=8)
     for tiles_ref, _, recv_ref in pairs:
         recv_ref[me] = tiles_ref[src_ref[me]]
 
@@ -373,7 +373,8 @@
     diag_ref, p_ref, inv_ref, pair_ref, col_ref, cols_ref,
     f_ref, c_ref, other_ref, hi_ref, lo_ref, w_ref, s_ref, base_ref, binv_ref,
     d_ref, dside_ref, dsend_ref, dside_send_ref, dgot_ref, dside_got_ref,
-    x_ref, xside_ref, out_ref, outside_ref, xsend_ref, xside_send_ref, xgot_ref, xside_got_ref, first_ref, a_ref, b_ref, t_ref,
+    x_ref, xside_ref, out_ref, outside_ref, xsend_ref, xside_send_ref, xgot_ref, xside_got_ref,
+    half_ref, halfside_ref, key_ref, keyside_ref, first_ref, a_ref, b_ref, t_ref,
     local, other_send, other_recv, dslot_send, dslot_recv, slot_send, slot_recv, half_send, half_recv,
     cols_send, cols_recv, first_send, first_recv, pair_send, pair_recv, col_send, col_recv,
 ):
@@ -469,27 +470,50 @@
     await_bytes(cols_ref.at[pl.ds(0, (panels - 1) * rows)], cols_recv)
     await_slots(total, x_pairs, slot_send, slot_recv)
     sum_cross(xindex_ref, xgot_ref, xside_got_ref, pair_ref, upper)
-    pair = to_panel(pair_ref.at[upper], pair_ref.at[upper], pair_send, pair_recv, panels // 2)
-    pair.start()
+    places = pair_ref.shape[1]
+    for r in range(places):
+        levels, level = to_levels(pair_ref[upper, r])
+        half_ref[upper, r] = levels
+        halfside_ref[upper, r] = level
+    pair = [
+        to_panel(ref.at[upper], ref.at[upper], pair_send.at[k], pair_recv.at[k], panels // 2)
+        for k, ref in enumerate((half_ref, halfside_ref))
+    ]
+    for copy in pair:
+        copy.start()
+
+    def take_pair():
+        for copy in pair:
+            copy.wait()
+        for r in range(places):
+            pair_ref[1 - upper, r] = from_levels(
+                half_ref[1 - upper, r], halfside_ref[1 - upper, r]
+            )
 
     @pl.when(panel % 2 == 0)
     def _():
-        key = pair_ref.at[upper, pl.ds(0, 2)]
         sends = [
-            to_panel(key, col_ref.at[upper], col_send.at[k], col_recv, away)
+            to_panel(
+                src.at[upper, pl.ds(0, 2)], dst.at[upper], col_send.at[2 * k + n], col_recv.at[n], away
+            )
             for k, away in enumerate((1, panels - 1))
+            for n, (src, dst) in enumerate(((half_ref, key_ref), (halfside_ref, keyside_ref)))
         ]
         for copy in sends:
             copy.start()
         for copy in sends:
             copy.wait_send()
-        pair.wait()
+        take_pair()
         col_ref[...] = pair_ref[:, :2]
 
     @pl.when(panel % 2 == 1)
     def _():
-        pair.wait()
-        await_bytes(col_ref, col_recv)
+        take_pair()
+        await_bytes(key_ref, col_recv.at[0])
+        await_bytes(keyside_ref, col_recv.at[1])
+        for n in range(2):
+            for r in range(2):
+                col_ref[n, r] = from_levels(key_ref[n, r], keyside_ref[n, r])
 
 
 def sum_diagonal(index_ref, recv_ref, side_ref, own_diag_ref, out_ref):
@@ -697,6 +721,10 @@
             VMEM((owners_total, 1, BLK), F32),
             VMEM((owners_total, HALF, BLK), I16),
             VMEM((owners_total, 1, BLK), F32),
+            VMEM((2, rows * rows, HALF, BLK), I16),
+            VMEM((2, rows * rows, 1, BLK), F32),
+            VMEM((2, 2, HALF, BLK), I16),
+            VMEM((2, 2, 1, BLK), F32),
             *[VMEM((BLK, BLK), F32)] * 4,
             dma((2,)),
             dma((subs,)),
@@ -705,9 +733,10 @@
             dma((panels - 1,)),
             dma,
             dma((panels - 1,)),
-            *[dma] * 3,
+            dma,
+            *[dma((2,))] * 2,
+            dma((4,)),
             dma((2,)),
-            dma,
         ],
         compiler_params=pltpu.CompilerParams(
             collective_id=1, has_side_effects=True, vmem_limit_bytes=50 * 2**20

time: 107 us -> 105 us (0.981); the launches traced: 106 us -> 105 us
  no operation moved by 1% of the time
where the time goes in v6:
time: 105 us
  Pallas kernels  100 us (95%)
  local copies, waits for them, and re-layouts  3.62 us (3%)
    pallas_call x1, Pallas kernels, per_device(): pl.pallas_call(whole_kernel, in_specs=[SMEM] * 4 + whole(2) + [anywhere]...  97.5 us
    pallas_call x1, Pallas kernels, per_device(): pl.pallas_call(final_kernel, in_specs=[SMEM] + whole(6), out_specs=whole(...  2.51 us
    unnamed x6, local copies, waits for them, and re-layouts  2.23 us

profile of v6, /device:TPU:8, one launch (start us, length us, event | category | flops | bytes accessed | tf_op | source)
XLA Modules:
  0.0 105.0 jit_solution(12261913187731091891)
XLA Ops:
  0.6 0.0 copy-start
  0.7 0.6 copy-done
  1.3 0.1 constant_dynamic-slice_fusion
  1.4 0.1 reshape.34.pat_ref
  1.5 1.1 %reshape.33 = s32[64,8,4,4]{1,0,3,2:T(8,128)S(1)} reshape(s32[512,16]{0,1:T(8,128)} %param.10) | data formatting | bytes 65536 | tf_op jit(solution)/shard_map/reshape | solution.py:666
  2.5 0.1 broadcast_compare_fusion
  2.7 0.2 add_select_fusion
  2.9 0.2 fusion.2
  3.0 0.1 copy.13
  3.1 0.1 eq.25
  3.2 0.1 select_reduce_fusion
  3.3 0.0 copy-start.1
  3.3 0.9 copy-done.1
  4.2 0.0 copy-start.2
  4.2 0.7 copy-done.2
  4.9 97.5 %whole.1 = (f32[2,128,128]{2,1,0:T(8,128)S(1)}, f32[128,128]{1,0:T(8,128)S(1)}, f32[128,128]{1,0:T(8,128)S(1)}, f32[2,4,64,128]{3,2,1,0:T(8,128)S(1)}, f32[2,2,6...) custom-call(s32[64]{0:T(128)S(1)} %broadcast_add_fusion.src_ref, s32[16]{0:T(128)S(1)} %reshape.34.pat_ref, ...), custom_call_target="tpu_custom_call" | custom-call | flops 10000000000 | bytes 16777216 | tf_op jit(solution)/shard_map/whole/pallas_call | solution.py:688
  102.4 2.5 %final.1 = (f32[256,1024]{1,0:T(8,128)}, f32[256,1024]{1,0:T(8,128)}) custom-call(s32[1]{0:T(128)} %bitcast.panel_ref, f32[2,128,128]{2,1,0:T(8,128)S(1)} %get-tuple-element.8.diag_ref, f32[2,4,64,128]{3,2,1,0:T(8,128)S(1)} %get-tuple-element.9.pair_ref, f32[2,2,64,128]{3,2,1,0:T(8,128)S(1)} %get-tuple-element.10.col_ref, ...), custom_call_target="tpu_custom_call" | custom-call | flops 1000000000 | bytes 4194304 | tf_op jit(solution)/shard_map/final/pallas_call | solution.py:750
  (3 shorter events, 0.0 us)
Async XLA Ops:
  0.6 0.7 copy-start
  3.3 0.9 copy-start.1
  4.2 0.7 copy-start.2

commit v7 on v6

--- a/solution.py
+++ b/solution.py
@@ -271,8 +271,8 @@
         act(sub_peer(step))
         return carry
 
-    lax.fori_loop(0, skip, one, 0)
-    lax.fori_loop(skip + 1, total, one, 0)
+    lax.fori_loop(0, skip, one, 0, unroll=7)
+    lax.fori_loop(skip + 1, total, one, 0, unroll=8)
 
 
 def greet(total, panels):

time: 105 us -> 105 us (level); the launches traced: 105 us -> 104 us
    pallas_call x1, Pallas kernels: 97.5 us -> 96.5 us  [per_device(): pl.pallas_call(whole_kernel, in_specs=[SMEM] * 4 + whole(2) + [anywhere]...]
where the time goes in v7:
time: 105 us; the launch traced here: 104 us
  Pallas kernels  99 us (94%)
  local copies, waits for them, and re-layouts  3.62 us (3%)
    pallas_call x1, Pallas kernels, per_device(): pl.pallas_call(whole_kernel, in_specs=[SMEM] * 4 + whole(2) + [anywhere]...  96.5 us
    pallas_call x1, Pallas kernels, per_device(): pl.pallas_call(final_kernel, in_specs=[SMEM] + whole(6), out_specs=whole(...  2.51 us
    unnamed x6, local copies, waits for them, and re-layouts  2.23 us

profile of v7, /device:TPU:8, one launch (start us, length us, event | category | flops | bytes accessed | tf_op | source)
XLA Modules:
  0.0 103.9 jit_solution(2250760803506373309)
XLA Ops:
  0.6 0.0 copy-start
  0.7 0.6 copy-done
  1.3 0.1 constant_dynamic-slice_fusion
  1.4 0.1 reshape.34.pat_ref
  1.5 1.1 %reshape.33 = s32[64,8,4,4]{1,0,3,2:T(8,128)S(1)} reshape(s32[512,16]{0,1:T(8,128)} %param.10) | data formatting | bytes 65536 | tf_op jit(solution)/shard_map/reshape | solution.py:666
  2.5 0.1 broadcast_compare_fusion
  2.7 0.2 add_select_fusion
  2.9 0.2 fusion.2
  3.0 0.1 copy.13
  3.1 0.1 eq.25
  3.2 0.1 select_reduce_fusion
  3.3 0.0 copy-start.1
  3.3 0.9 copy-done.1
  4.2 0.0 copy-start.2
  4.2 0.7 copy-done.2
  4.9 96.5 %whole.1 = (f32[2,128,128]{2,1,0:T(8,128)S(1)}, f32[128,128]{1,0:T(8,128)S(1)}, f32[128,128]{1,0:T(8,128)S(1)}, f32[2,4,64,128]{3,2,1,0:T(8,128)S(1)}, f32[2,2,6...) custom-call(s32[64]{0:T(128)S(1)} %broadcast_add_fusion.src_ref, s32[16]{0:T(128)S(1)} %reshape.34.pat_ref, ...), custom_call_target="tpu_custom_call" | custom-call | flops 10000000000 | bytes 16777216 | tf_op jit(solution)/shard_map/whole/pallas_call | solution.py:688
  101.4 2.5 %final.1 = (f32[256,1024]{1,0:T(8,128)}, f32[256,1024]{1,0:T(8,128)}) custom-call(s32[1]{0:T(128)} %bitcast.panel_ref, f32[2,128,128]{2,1,0:T(8,128)S(1)} %get-tuple-element.8.diag_ref, f32[2,4,64,128]{3,2,1,0:T(8,128)S(1)} %get-tuple-element.9.pair_ref, f32[2,2,64,128]{3,2,1,0:T(8,128)S(1)} %get-tuple-element.10.col_ref, ...), custom_call_target="tpu_custom_call" | custom-call | flops 1000000000 | bytes 4194304 | tf_op jit(solution)/shard_map/final/pallas_call | solution.py:750
  (3 shorter events, 0.0 us)
Async XLA Ops:
  0.6 0.7 copy-start
  3.3 0.9 copy-start.1
  4.2 0.7 copy-start.2
